TPU v7x, 256 devices: a whole 4x4x8 slice. The times are simulated.
256 devices in a mesh: ga: 256 (over z, y, x, core).
Axes of the slice: x: 4, y: 4, z: 8, core: 2. Of those that a mesh axis runs over, the one named last changes fastest.
Arguments:
- text_states: bfloat16 [4096, 512], P('ga')
- text_proj: bfloat16 [512, 1024], replicated
- gallery: bfloat16 [131072, 1024], P('ga')
- logit_scale: float32 [1], replicated
Outputs:
- output 1: bfloat16 [4096, 131072], P(None, 'ga')
- output 2: float32 [4096], replicated
All inputs are finite; a program needn't handle non-finite values.
Results may differ from a plain program's by a relative error of at most 0.0023.
Values are sent between devices in bfloat16 or wider.
A program may use at most 768 MiB of HBM per device.

v0:
```python
import jax
import jax.numpy as jnp
from jax import lax
from jax.sharding import PartitionSpec as P, NamedSharding


def solution(mesh):
    num_dev = mesh.shape["ga"]

    def per_device(text_states, text_proj, gallery, logit_scale):
        proj_out = jnp.dot(text_states, text_proj, preferred_element_type=jnp.float32)
        unit_q = proj_out / jnp.sqrt(jnp.sum(proj_out * proj_out, axis=1, keepdims=True))
        query_emb = unit_q.astype(jnp.bfloat16)
        all_queries = lax.all_gather(query_emb, "ga", axis=0, tiled=True)
        logit_mult = jnp.exp(logit_scale[0])
        scores = logit_mult * lax.dot_general(all_queries, gallery, (((1,), (1,)), ((), ())),
                                              preferred_element_type=jnp.float32)
        glob_max = lax.pmax(jnp.max(scores, axis=1), "ga")
        exp_vals = jnp.exp(scores - glob_max[:, None])
        glob_sum = lax.psum(jnp.sum(exp_vals, axis=1), "ga")
        prob_vals = exp_vals / glob_sum[:, None]
        local_rows = gallery.shape[0]
        total_rows = local_rows * num_dev
        row_ids = lax.axis_index("ga") * local_rows + jnp.arange(local_rows, dtype=jnp.int32)
        positions = row_ids.astype(jnp.float32) / total_rows
        exp_rank = lax.psum(jnp.sum(prob_vals * positions, axis=1), "ga")
        return prob_vals.astype(jnp.bfloat16), exp_rank

    return jax.shard_map(per_device, mesh=mesh,
                         in_specs=(P("ga", None), P(None, None), P("ga", None), P(None)),
                         out_specs=(P(None, "ga"), P(None)), check_vma=False)
```

profile of v0, /device:TPU:1, one launch (start us, length us, event | category | flops | bytes accessed | tf_op | source)
XLA Modules:
  0.0 390.4 jit_solution(2579547433419160713)
XLA Ops:
  7.2 0.0 copy-start
  7.2 0.0 all-gather.2.cloned.1.call-start
  7.2 1.7 multiply_reduce_fusion.2
  8.9 0.7 divide_convert_fusion
  9.6 0.0 all-gather.2.cloned.1.call-update
  10.4 123.8 %all-gather.2.cloned.1.call-done = bf16[4096,1024]{1,0:T(8,128)(2,1)} async-done(((bf16[16,1024]{1,0:T(8,128)(2,1)}), bf16[4096,1024]{1,0:T(8,128)(2,1)}) %all-gather.2.cloned.1.call-update) | async-done | bytes 8388624 | tf_op jit(solution)/shard_map/all_gather | solution.py:14
  134.2 0.0 copy-done
  134.2 10.1 %multiply_reduce_fusion.1 = (f32[4096]{0:T(1024)S(1)}, f32[4096,512]{0,1:T(8,128)}) fusion(f32[]{:T(128)} %bitcast, bf16[4096,1024]{1,0:T(8,128)(2,1)} %all-gather.2.cloned.1.call-done, bf16[512,1024]{1,0:T(8,128)(2,1)S(1)} %copy-done), kind=kOutput, calls=%fused_computation.2 | convolution fusion | flops 4299157504 | bytes 17842180 | tf_op jit(solution)/shard_map/dot_general | solution.py:16
  144.3 74.5 %pmax.7 = f32[4096]{0:T(1024)S(1)} all-reduce(f32[4096]{0:T(1024)S(1)} %get-tuple-element.8), channel_id=1, replica_groups=mesh['ga'=256] {'ga'}, use_global_device_ids=true, to_apply=%region_2.0 | all-reduce | flops 4096 | bytes 32768 | tf_op jit(solution)/shard_map/pmax | solution.py:18
  218.8 4.8 %fusion.1 = f32[4096]{0:T(1024)S(1)} fusion(f32[4096,512]{0,1:T(8,128)} %get-tuple-element.9, f32[4096]{0:T(1024)S(1)} %pmax.7, f32[]{:T(128)} %bitcast), kind=kLoop, calls=%fused_computation.4 | loop fusion | flops 6287360 | bytes 8421380 | tf_op jit(solution)/shard_map/reduce_sum | solution.py:20
  223.6 73.9 %psum.14 = f32[4096]{0:T(1024)S(1)} all-reduce(f32[4096]{0:T(1024)S(1)} %fusion.1), channel_id=1, replica_groups=mesh['ga'=256] {'ga'}, use_global_device_ids=true, to_apply=%region_4.0 | all-reduce | flops 4096 | bytes 32768 | tf_op jit(solution)/shard_map/psum | solution.py:20
  297.5 5.9 %multiply_reduce_fusion = (f32[4096]{0:T(1024)S(1)}, bf16[4096,512]{0,1:T(8,128)(2,1)}) fusion(f32[512]{0:T(512)S(1)} %convert_multiply_fusion, f32[4096]{0:T(1024)S(1)} %psum.14, f32[4096]{0:T(1024)S(1)} %pmax.7, f32[4096,512]{0,1:T(8,128)} %get-tuple-element.9, f32[]{:T(128)} %bitcast), kind=kLoop, calls=%fused_computation | loop fusion | flops 12578816 | bytes 12634116 | tf_op jit(solution)/shard_map/reduce_sum | solution.py:26
  303.3 6.4 %copy.6 = bf16[4096,512]{1,0:T(8,128)(2,1)} copy(bf16[4096,512]{0,1:T(8,128)(2,1)} %get-tuple-element.5) | data formatting | bytes 8388608
  309.7 73.8 %psum.15 = f32[4096]{0:T(1024)} all-reduce(f32[4096]{0:T(1024)S(1)} %get-tuple-element.4), channel_id=1, replica_groups=mesh['ga'=256] {'ga'}, use_global_device_ids=true, to_apply=%region_6.0 | all-reduce | flops 4096 | bytes 32768 | tf_op jit(solution)/shard_map/psum | solution.py:26
  (2 shorter events, 0.0 us)
Async XLA Ops:
  7.2 127.0 %copy-start = (bf16[512,1024]{1,0:T(8,128)(2,1)S(1)}, bf16[512,1024]{1,0:T(8,128)(2,1)}, u32[]{:S(2)}) copy-start(bf16[512,1024]{1,0:T(8,128)(2,1)} %param.6) | copy-start | bytes 3145732
  7.2 127.0 %all-gather.2.cloned.1.call-start = ((), (), s32[]{:S(2)}) async-start(), calls=%async_computation | async-start | bytes 8421376 | tf_op jit(solution)/shard_map/all_gather | solution.py:14
Sparse Core Ops, SparseCore 0:
  12.1 122.0 all-gather.1
where the time goes:
time: 391 us; the launch traced here: 390 us
  blocking collectives  222 us (57%)
  waiting for transfers between devices  124 us (32%)
  between operations  14.7 us (4%)
  matrix products  11.8 us (3%)
  other arithmetic  11.3 us (3%)
  local copies, waits for them, and re-layouts  6.42 us (2%)
    all_gather x1, waiting for transfers between devices, per_device(): all_queries = lax.all_gather(query_emb, 'ga', axis=0, tiled=True)  124 us
    pmax x1, blocking collectives, per_device(): glob_max = lax.pmax(jnp.max(scores, axis=1), 'ga')  74.5 us
    psum x1, blocking collectives, per_device(): glob_sum = lax.psum(jnp.sum(exp_vals, axis=1), 'ga')  73.9 us
    psum x1, blocking collectives, per_device(): exp_rank = lax.psum(jnp.sum(prob_vals * positions, axis=1), 'ga')  73.8 us
    dot_general x1, matrix products, per_device(): lax.dot_general(all_queries, gallery, (((1,), (1,)), ((), ())), preferred...  10.1 us
  transfers between devices with their start and end apart: 1, of which 1 were waited for; matrix products, arithmetic and copies ran while one was open for 0% of the time, Pallas kernels for 0%

commit v1 on v0

v1 whole, which is shorter than its diff:
```python
import functools

import jax
import jax.numpy as jnp
from jax import lax
from jax.experimental import pallas as pl
from jax.experimental.pallas import tpu as pltpu
from jax.sharding import PartitionSpec as P

MESH = pl.DeviceIdType.MESH
NX, NY, NZ, NC = 4, 4, 8, 2
F32, BF16 = jnp.float32, jnp.bfloat16


def gather_score_kernel(x_hbm, w_hbm, g_hbm, t_ref,
                        e_ref, fac_ref, rank_ref,
                        xs, wv, gv, stat, part, zpart, done,
                        in_sem, x_send, x_recv, y_send, y_recv,
                        r_send, r_recv, l_send, l_recv, d_send, d_recv,
                        s1_send, s1_recv, s2_send, s2_recv, s3_send, s3_recv):
    me = lax.axis_index("ga")
    c = lax.rem(me, NC)
    x = lax.rem(me // 2, NX)
    y = lax.rem(me // 8, NY)
    z = me // 32
    pi = lax.rem(me, 32)

    def dev(zz, yy, xx, cc):
        return ((zz * NY + yy) * NX + xx) * NC + cc

    load_x = pltpu.make_async_copy(x_hbm, xs.at[z, y, x, c], in_sem.at[0])
    load_w = pltpu.make_async_copy(w_hbm, wv, in_sem.at[1])
    load_g = pltpu.make_async_copy(g_hbm, gv, in_sem.at[2])
    load_x.start()
    load_w.start()
    load_g.start()

    zr = lax.rem(z + 1, NZ)
    zl = lax.rem(z + NZ - 1, NZ)
    sib = dev(z, y, x, 1 - c)
    x_peers = [dev(z, y, lax.rem(x + d, NX), c) for d in range(1, NX)]
    y_peers = [dev(z, lax.rem(y + d, NY), x, c) for d in range(1, NY)]
    right, left = dev(zr, y, x, c), dev(zl, y, x, c)

    barrier = pltpu.get_barrier_semaphore()
    for p in [sib, right, left] + x_peers + y_peers:
        pl.semaphore_signal(barrier, inc=1, device_id=(p,), device_id_type=MESH)
    pl.semaphore_wait(barrier, 9)
    load_x.wait()

    def rcopy(src, dst, ss, rs, p):
        return pltpu.make_async_remote_copy(src_ref=src, dst_ref=dst, send_sem=ss, recv_sem=rs,
                                            device_id=(p,), device_id_type=MESH)

    own = xs.at[z, y, x, c]
    for d in range(1, NX):
        rcopy(own, own, x_send.at[d - 1], x_recv.at[d - 1], x_peers[d - 1]).start()

    def row(zz, j):
        return xs.at[zz, lax.rem(y + j, NY), :, c]

    def to_right(zz, s, j):
        return rcopy(row(zz, j), row(zz, j), r_send.at[s * 4 + j], r_recv.at[s * 4 + j], right)

    def to_left(zz, s, j):
        return rcopy(row(zz, j), row(zz, j), l_send.at[s * 4 + j], l_recv.at[s * 4 + j], left)

    def to_sib(zz, p, j):
        return rcopy(row(zz, j), row(zz, j), d_send.at[p * 4 + j], d_recv.at[p * 4 + j], sib)

    for d in range(1, NX):
        rcopy(own, own, x_send.at[d - 1], x_recv.at[d - 1], x_peers[d - 1]).wait_recv()
    my_row = row(z, 0)
    for d in range(1, NY):
        rcopy(my_row, my_row, y_send.at[d - 1], y_recv.at[NY - d - 1], y_peers[d - 1]).start()
    to_right(z, 0, 0).start()
    to_left(z, 0, 0).start()
    to_sib(z, 0, 0).start()
    for j in range(1, NY):
        rcopy(row(z, j), row(z, j), y_send.at[0], y_recv.at[j - 1], sib).wait_recv()
        to_right(z, 0, j).start()
        to_left(z, 0, j).start()
        to_sib(z, 0, j).start()

    load_w.wait()
    load_g.wait()
    mult = jnp.exp(t_ref[...])
    col = lax.broadcasted_iota(jnp.int32, (1, 512), 1) + me * 512
    pos = col.astype(F32) / (256 * 512.0)
    lane = lax.broadcasted_iota(jnp.int32, (256, 128), 1)

    def unit(u):
        a = u - 2
        s = a // 4
        jr = lax.rem(jnp.maximum(a, 0), 4)
        head = u < 2
        last = u >= 14
        z1 = jnp.where(head, z, lax.rem(z + 2 * NZ - 1 - s, NZ))
        z2 = jnp.where(head, z, lax.rem(z + 1 + s, NZ))
        j1 = jnp.where(head, 2 * u, jr)
        j2 = jnp.where(head, 2 * u + 1, jnp.where(last, jr + 2, jr))
        p1 = jnp.where(head, 0, jnp.where(last, 7, 1 + s))
        p2 = jnp.where(head, 0, jnp.where(last, 7, 4 + s))
        return (z1, j1, p1), (z2, j2, p2)

    def wait_sib(zz, p, j):
        other = xs.at[zz, lax.rem(y + j, NY), :, 1 - c]
        rcopy(other, other, d_send.at[p * 4 + j], d_recv.at[p * 4 + j], sib).wait_recv()

    def owner_copy(gq):
        return rcopy(stat.at[gq], part.at[pi], s1_send.at[gq], s1_recv.at[pi], z * 32 + gq)

    def send_stats(u):
        for zz, j, _ in unit(u):
            gq = zz * 4 + lax.rem(y + j, NY)

            @pl.when(gq != pi)
            def _():
                owner_copy(gq).start()

            @pl.when(gq == pi)
            def _():
                part[pi] = stat[pi]

    def compute(u):
        (z1, j1, p1), (z2, j2, p2) = unit(u)
        wait_sib(z1, p1, j1)
        wait_sib(z2, p2, j2)
        y1, y2 = lax.rem(y + j1, NY), lax.rem(y + j2, NY)
        rows = jnp.concatenate([xs[z1, y1].reshape(128, 512), xs[z2, y2].reshape(128, 512)], axis=0)
        proj = jnp.dot(rows, wv[...], preferred_element_type=F32)
        inv = 1.0 / jnp.sqrt(jnp.sum(proj * proj, axis=1, keepdims=True))
        q = (proj * inv).astype(BF16)
        sc = mult * lax.dot_general(q, gv[...], (((1,), (1,)), ((), ())), preferred_element_type=F32)
        m = jnp.max(sc, axis=1, keepdims=True)
        ev = jnp.exp(sc - m)
        zs = jnp.sum(ev, axis=1, keepdims=True)
        rs = jnp.sum(ev * pos, axis=1, keepdims=True)
        e_ref[z1 * 4 + y1] = ev[:128]
        e_ref[z2 * 4 + y2] = ev[128:]
        cols = jnp.where(lane == 0, m, jnp.where(lane == 1, zs, rs))
        stat[z1 * 4 + y1] = cols[:128].T[:8]
        stat[z2 * 4 + y2] = cols[128:].T[:8]

    def body(i, carry):
        @pl.when(i < 14)
        def _():
            s = i // 4
            j1 = lax.rem(i, 4)
            j2 = jnp.where(i >= 12, j1 + 2, j1)
            z1 = lax.rem(z + 2 * NZ - 1 - s, NZ)
            z2 = lax.rem(z + 1 + s, NZ)
            to_right(z1, s, j1).wait_recv()

            @pl.when(jnp.logical_or(i < 8, jnp.logical_and(i < 12, j1 < 2)))
            def _():
                to_right(z1, s + 1, j1).start()

            to_sib(z1, jnp.where(i >= 12, 7, 1 + s), j1).start()
            to_left(z2, s, j2).wait_recv()

            @pl.when(jnp.logical_or(i < 8, jnp.logical_and(i < 12, j2 >= 2)))
            def _():
                to_left(z2, s + 1, j2).start()

            to_sib(z2, jnp.where(i >= 12, 7, 4 + s), j2).start()

        compute(i)

        @pl.when(i >= 1)
        def _():
            send_stats(i - 1)

        return carry

    lax.fori_loop(0, 16, body, 0)
    send_stats(15)

    def wait_part(k, carry):
        @pl.when(k != pi)
        def _():
            rcopy(part.at[k], part.at[k], s1_send.at[0], s1_recv.at[k], sib).wait_recv()
        return carry

    lax.fori_loop(0, 32, wait_part, 0)

    def merge(ref):
        ms = ref[:, 0, :]
        m = jnp.max(ms, axis=0, keepdims=True)
        wgt = jnp.exp(ms - m)
        return m, jnp.sum(wgt * ref[:, 1, :], axis=0, keepdims=True), jnp.sum(wgt * ref[:, 2, :], axis=0, keepdims=True)

    sub = lax.broadcasted_iota(jnp.int32, (8, 128), 0)

    def tile(a, b, d):
        return jnp.where(sub == 0, a, jnp.where(sub == 1, b, d))

    t1 = tile(*merge(part))
    zpart[z] = t1
    z_peers = [dev(lax.rem(z + d, NZ), y, x, c) for d in range(1, NZ)]
    for d in range(1, NZ):
        rcopy(zpart.at[z], zpart.at[z], s2_send.at[d - 1], s2_recv.at[NZ - d - 1], z_peers[d - 1]).start()
    for d in range(1, NZ):
        zz = lax.rem(z + d, NZ)
        rcopy(zpart.at[zz], zpart.at[zz], s2_send.at[d - 1], s2_recv.at[d - 1], sib).wait_recv()
    m, zs, rs = merge(zpart)
    done[pi] = tile(m, 1.0 / zs, rs / zs)

    def send_done(k, carry):
        p = lax.rem(pi + k, 32)
        rcopy(done.at[pi], done.at[pi], s3_send.at[k - 1], s3_recv.at[31 - k], z * 32 + p).start()
        return carry

    lax.fori_loop(1, 32, send_done, 0)

    def wait_done(k, carry):
        p = lax.rem(pi + k, 32)
        rcopy(done.at[p], done.at[p], s3_send.at[k - 1], s3_recv.at[k - 1], sib).wait_recv()
        return carry

    lax.fori_loop(1, 32, wait_done, 0)
    fac_ref[...] = jnp.exp(stat[:, 0, :] - done[:, 0, :]) * done[:, 1, :]
    rank_ref[...] = done[:, 2, :]

    for d in range(1, NX):
        rcopy(own, own, x_send.at[d - 1], x_recv.at[d - 1], sib).wait_send()
        rcopy(my_row, my_row, y_send.at[d - 1], y_recv.at[d - 1], sib).wait_send()
    for d in range(1, NZ):
        rcopy(zpart.at[z], zpart.at[z], s2_send.at[d - 1], s2_recv.at[d - 1], sib).wait_send()

    def drain(k, carry):
        rcopy(my_row, my_row, d_send.at[k], d_recv.at[k], sib).wait_send()

        @pl.when(k < 14)
        def _():
            rcopy(my_row, my_row, r_send.at[k], r_recv.at[k], sib).wait_send()

        @pl.when(jnp.logical_or(k < 12, jnp.logical_and(k >= 14, k < 16)))
        def _():
            rcopy(my_row, my_row, l_send.at[k], l_recv.at[k], sib).wait_send()

        @pl.when(k != pi)
        def _():
            rcopy(stat.at[k], part.at[k], s1_send.at[k], s1_recv.at[k], sib).wait_send()

        @pl.when(k < 31)
        def _():
            rcopy(stat.at[k], part.at[k], s3_send.at[k], s3_recv.at[k], sib).wait_send()
        return carry

    lax.fori_loop(0, 32, drain, 0)


def normalise_kernel(e_ref, fac_ref, rank_ref, p_ref, r_ref):
    i = pl.program_id(0)

    def body(k, carry):
        gq = i * 4 + k
        f = jnp.broadcast_to(fac_ref[pl.ds(gq, 1), :], (128, 128)).T
        ev = e_ref[gq]
        for b in range(4):
            p_ref[pl.ds(k * 128, 128), b * 128:(b + 1) * 128] = (ev[:, b * 128:(b + 1) * 128] * f).astype(BF16)
        return carry

    lax.fori_loop(0, 4, body, 0)
    r_ref[...] = rank_ref[...]


def solution(mesh):
    D = pltpu.SemaphoreType.DMA
    VM = pltpu.VMEM

    def per_device(text_states, text_proj, gallery, logit_scale):
        e, fac, rank = pl.pallas_call(
            gather_score_kernel,
            out_shape=(VM((32, 128, 512), F32), VM((32, 128), F32), VM((32, 128), F32)),
            in_specs=[pl.BlockSpec(memory_space=pl.ANY)] * 3 + [pl.BlockSpec(memory_space=VM)],
            out_specs=(pl.BlockSpec(memory_space=VM),) * 3,
            scratch_shapes=[
                VM((NZ, NY, NX, NC, 16, 512), BF16), VM((512, 1024), BF16), VM((512, 1024), BF16),
                VM((32, 8, 128), F32), VM((32, 8, 128), F32), VM((NZ, 8, 128), F32),
                VM((32, 8, 128), F32),
                D((3,)), D((3,)), D((3,)), D((3,)), D((3,)),
                D((16,)), D((16,)), D((16,)), D((16,)), D((32,)), D((32,)),
                D((32,)), D((32,)), D((7,)), D((7,)), D((31,)), D((31,)),
            ],
            compiler_params=pltpu.CompilerParams(collective_id=0, has_side_effects=True,
                                                 vmem_limit_bytes=48 * 1024 * 1024),
        )(text_states, text_proj, gallery, logit_scale.reshape(1, 1))
        prob, rank = pl.pallas_call(
            normalise_kernel,
            grid=(8,),
            out_shape=(jax.ShapeDtypeStruct((4096, 512), BF16), jax.ShapeDtypeStruct((32, 128), F32)),
            in_specs=[pl.BlockSpec(memory_space=VM)] * 3,
            out_specs=(pl.BlockSpec((512, 512), lambda i: (i, 0)), pl.BlockSpec((32, 128), lambda i: (0, 0))),
            compiler_params=pltpu.CompilerParams(vmem_limit_bytes=24 * 1024 * 1024),
        )(e, fac, rank)
        return prob, rank.reshape(4096)

    return jax.shard_map(per_device, mesh=mesh,
                         in_specs=(P("ga", None), P(None, None), P("ga", None), P(None)),
                         out_specs=(P(None, "ga"), P(None)), check_vma=False)
```

time: 391 us -> 64.4 us (0.16)
  blocking collectives: 222 us -> 0 us
  waiting for transfers between devices: 124 us -> 0 us
  Pallas kernels: 0 us -> 63.1 us
  between operations: 14.7 us -> 1.28 us
  matrix products: 11.8 us -> 0 us
  other arithmetic: 11.3 us -> 0 us
  local copies, waits for them, and re-layouts: 6.42 us -> 0 us
    psum x2 -> x0, blocking collectives: 148 us -> none  [the longest x1 73.9 us: per_device(): glob_sum = lax.psum(jnp.sum(exp_vals, axis=1), 'ga')]
    all_gather x1 -> x0, waiting for transfers between devices: 124 us -> none  [per_device(): all_queries = lax.all_gather(query_emb, 'ga', axis=0, tiled=True)]
    pmax x1 -> x0, blocking collectives: 74.5 us -> none  [per_device(): glob_max = lax.pmax(jnp.max(scores, axis=1), 'ga')]
    pallas_call x0 -> x2, Pallas kernels: none -> 63.1 us  [the longest x1 57.8 us: per_device(): pl.pallas_call(gather_score_kernel, out_shape=(VM((32, 128, 512), F32), V...]
    dot_general x2 -> x0, matrix products: 11.8 us -> none  [the longest x1 10.1 us: per_device(): lax.dot_general(all_queries, gallery, (((1,), (1,)), ((), ())), preferred...]
    reduce_sum x2 -> x0, other arithmetic: 10.6 us -> none  [the longest x1 5.86 us: per_device(): exp_rank = lax.psum(jnp.sum(prob_vals * positions, axis=1), 'ga')]
    unnamed x3 -> x0, local copies, waits for them, and re-layouts: 6.41 us -> none
  transfers between devices with their start and end apart: 1 -> 0, of which waited for: 1 -> 0; matrix products, arithmetic and copies ran while one was open for 0% -> 0% of each run, Pallas kernels for 0% -> 0%
where the time goes in v1:
time: 64.4 us; the launch traced here: 64.3 us
  Pallas kernels  63.1 us (98%)
  between operations  1.28 us (2%)
    pallas_call x1, Pallas kernels, per_device(): pl.pallas_call(gather_score_kernel, out_shape=(VM((32, 128, 512), F32), V...  57.8 us
    pallas_call x1, Pallas kernels, per_device(): pl.pallas_call(normalise_kernel, grid=(8,), out_shape=(jax.ShapeDtypeStru...  5.26 us

profile of v1, /device:TPU:1, one launch (start us, length us, event | category | flops | bytes accessed | tf_op | source)
XLA Modules:
  0.0 64.3 jit_solution(10598991823736571428)
XLA Ops:
  1.3 57.8 %shard_map.59 = (f32[32,128,512]{2,1,0:T(8,128)S(1)}, f32[32,128]{1,0:T(8,128)S(1)}, f32[32,128]{1,0:T(8,128)S(1)}) custom-call(bf16[16,512]{1,0:T(8,128)(2,1)} %x_hbm.1, bf16[512,1024]{1,0:T(8,128)(2,1)} %w_hbm.1, bf16[512,1024]{1,0:T(8,128)(2,1)} %g_hbm.1, f32[1,1]{1,0:T(1,128)} %bitcast.2.t_ref), custom_call_target="tpu_custom_call" | custom-call | tf_op jit(solution)/shard_map/pallas_call | solution.py:274
  59.1 5.3 %shard_map.60 = (bf16[4096,512]{1,0:T(8,128)(2,1)}, f32[32,128]{1,0:T(8,128)}) custom-call(f32[32,128,512]{2,1,0:T(8,128)S(1)} %get-tuple-element.7.e_ref, f32[32,128]{1,0:T(8,128)S(1)} %get-tuple-element.8.fac_ref, f32[32,128]{1,0:T(8,128)S(1)} %get-tuple-element.9.rank_ref), custom_call_target="tpu_custom_call" | custom-call | tf_op jit(solution)/shard_map/pallas_call | solution.py:290

commit v2 on v0

v2 whole, which is shorter than its diff:
```python
import jax
import jax.numpy as jnp
from jax import lax
from jax.experimental import pallas as pl
from jax.experimental.pallas import tpu as pltpu
from jax.sharding import PartitionSpec as P

MESH = pl.DeviceIdType.MESH
NX, NY, NZ, NC = 4, 4, 8, 2
F32, BF16 = jnp.float32, jnp.bfloat16
LOG2E = 1.4426950408889634
F32_MAX = 3.4028235e38
scope = jax.named_scope


def rcopy(src, dst, ss, rs, p):
    return pltpu.make_async_remote_copy(src_ref=src, dst_ref=dst, send_sem=ss, recv_sem=rs,
                                        device_id=(p,), device_id_type=MESH)


def gather_score_kernel(x_hbm, w_hbm, g_hbm, t_ref,
                        e_ref, fac_ref, rank_ref,
                        xs, wv, gv, qown, qsib, stat, part, zpart, done,
                        in_sem, a_send, a_recv, y_send, y_recv,
                        r_send, r_recv, l_send, l_recv, q_send, q_recv,
                        s1_send, s1_recv, s2_send, s2_recv, s3_send, s3_recv):
    me = lax.axis_index("ga")
    c = lax.rem(me, NC)
    x = lax.rem(me // 2, NX)
    y = lax.rem(me // 8, NY)
    z = me // 32
    pi = lax.rem(me, 32)
    core0, core1 = c == 0, c == 1

    def dev(zz, yy, xx, cc):
        return ((zz * NY + yy) * NX + xx) * NC + cc

    def own_block():
        return (jnp.where(core0, z, 2 * x + z // 4), jnp.where(core0, y, lax.rem(z, 4)), jnp.where(core0, x, y))

    u0, u1, u2 = own_block()
    own = xs.at[u0, u1, u2]
    load_x = pltpu.make_async_copy(x_hbm, own, in_sem.at[0])
    load_w = pltpu.make_async_copy(w_hbm, wv, in_sem.at[1])
    load_g = pltpu.make_async_copy(g_hbm, gv, in_sem.at[2])
    load_x.start()
    load_w.start()
    load_g.start()

    sib = dev(z, y, x, 1 - c)
    x_peers = [dev(z, y, lax.rem(x + d, NX), c) for d in range(1, NX)]
    y_peers = [dev(z, lax.rem(y + d, NY), x, c) for d in range(1, NY)]
    z_peers = [dev(lax.rem(z + d, NZ), y, x, c) for d in range(1, NZ)]

    barrier = pltpu.get_barrier_semaphore()

    def greet(peers):
        for p in peers:
            pl.semaphore_signal(barrier, inc=1, device_id=(p,), device_id_type=MESH)
        pl.semaphore_wait(barrier, len(peers))

    with scope("barrier"):
        @pl.when(core0)
        def _():
            greet([sib] + x_peers + y_peers + [z_peers[0], z_peers[-1]])

        @pl.when(core1)
        def _():
            greet([sib] + z_peers + y_peers + [x_peers[0], x_peers[-1]])

        load_x.wait()

    def row(zz, j):
        return xs.at[zz, lax.rem(y + j, NY)]

    def a_right(zz, k, j):
        return rcopy(row(zz, j), row(zz, j), r_send.at[k], r_recv.at[k], z_peers[0])

    def a_left(zz, k, j):
        return rcopy(row(zz, j), row(zz, j), l_send.at[k], l_recv.at[k], z_peers[-1])

    @pl.when(core0)
    def _():
        for d in range(1, NX):
            rcopy(own, own, a_send.at[d - 1], a_recv.at[d - 1], x_peers[d - 1]).start()
        with scope("first"):
            for d in range(1, NX):
                rcopy(own, own, a_send.at[d - 1], a_recv.at[d - 1], x_peers[d - 1]).wait_recv()
        for d in range(1, NY):
            rcopy(row(z, 0), row(z, 0), y_send.at[d - 1], y_recv.at[NY - d - 1], y_peers[d - 1]).start()
        a_right(z, 0, 0).start()
        a_left(z, 0, 0).start()
        for j in range(1, NY):
            with scope("second"):
                rcopy(row(z, j), row(z, j), y_send.at[0], y_recv.at[j - 1], sib).wait_recv()
            a_right(z, j, j).start()
            a_left(z, j, j).start()

    def a_event(e, carry):
        s = e // 4
        j1 = lax.rem(e, 4)
        j2 = jnp.where(e >= 12, j1 + 2, j1)
        z1 = lax.rem(z + 2 * NZ - 1 - s, NZ)
        z2 = lax.rem(z + 1 + s, NZ)
        a_right(z1, s * 4 + j1, j1).wait_recv()

        @pl.when(jnp.logical_or(e < 8, jnp.logical_and(e < 12, j1 < 2)))
        def _():
            a_right(z1, s * 4 + 4 + j1, j1).start()

        a_left(z2, s * 4 + j2, j2).wait_recv()

        @pl.when(jnp.logical_or(e < 8, jnp.logical_and(e < 12, j2 >= 2)))
        def _():
            a_left(z2, s * 4 + 4 + j2, j2).start()

        return carry

    def piece(xx, h, j):
        return xs.at[2 * xx + h, :, lax.rem(y + j, NY)]

    def b_right(xx, h, k, j):
        return rcopy(piece(xx, h, j), piece(xx, h, j), r_send.at[k], r_recv.at[k], x_peers[0])

    def b_left(xx, h, k, j):
        return rcopy(piece(xx, h, j), piece(xx, h, j), l_send.at[k], l_recv.at[k], x_peers[-1])

    @pl.when(core1)
    def _():
        for d in range(1, NZ):
            rcopy(own, own, a_send.at[d - 1], a_recv.at[NZ - d - 1], z_peers[d - 1]).start()
        with scope("first"):
            for d in range(1, NZ):
                rcopy(own, own, a_send.at[d - 1], a_recv.at[d - 1], z_peers[d - 1]).wait_recv()
        for h in range(2):
            for d in range(1, NY):
                rcopy(piece(x, h, 0), piece(x, h, 0), y_send.at[h * 3 + d - 1], y_recv.at[h * 3 + NY - d - 1],
                      y_peers[d - 1]).start()
            b_right(x, h, h * 4, 0).start()
            b_left(x, h, h * 4, 0).start()
        for h in range(2):
            for j in range(1, NY):
                with scope("second"):
                    rcopy(piece(x, h, j), piece(x, h, j), y_send.at[0], y_recv.at[h * 3 + j - 1], sib).wait_recv()
                b_right(x, h, h * 4 + j, j).start()
                b_left(x, h, h * 4 + j, j).start()

    def b_event(e, carry):
        j = lax.rem(e, 4)
        far = e >= 8
        xr = jnp.where(far, lax.rem(x + 2, NX), lax.rem(x + 3, NX))
        xl = jnp.where(far, lax.rem(x + 2, NX), lax.rem(x + 1, NX))
        hr = jnp.where(far, 0, e // 4)
        hl = jnp.where(far, 1, e // 4)
        b_right(xr, hr, e, j).wait_recv()

        @pl.when(e < 4)
        def _():
            b_right(xr, hr, 8 + j, j).start()

        b_left(xl, hl, e, j).wait_recv()

        @pl.when(jnp.logical_and(e >= 4, e < 8))
        def _():
            b_left(xl, hl, 8 + j, j).start()

        return carry

    def events(k):
        with scope("events"):
            @pl.when(core0)
            def _():
                lo = jnp.where(k == 1, 0, jnp.minimum(2 * k, k + 6))
                hi = jnp.minimum(2 * k + 2, k + 7)
                lax.fori_loop(lo, hi, a_event, 0)

            @pl.when(core1)
            def _():
                lax.fori_loop(jnp.minimum(2 * k - 2, 12), jnp.minimum(2 * k, 12), b_event, 0)

    def unit_of(cc0, u):
        odd = lax.rem(u, 2) == 1
        dz = jnp.where(odd, -((u + 1) // 2), (u + 1) // 2)
        za = lax.rem(z + dz + 2 * NZ, NZ)
        dx = jnp.where(u < 2, 0, jnp.where(u >= 6, 2, jnp.where(odd, 1, NX - 1)))
        h = jnp.where(u < 2, u, jnp.where(u >= 6, u - 6, (u - 2) // 2))
        ub = 2 * lax.rem(x + dx, NX) + h
        return jnp.where(cc0, za, ub), jnp.where(cc0, 2 * za, 16 + 2 * ub)

    load_w.wait()
    load_g.wait()
    k2 = jnp.minimum(jnp.exp(t_ref[...]) * LOG2E, F32_MAX)
    col = lax.broadcasted_iota(jnp.int32, (1, 512), 1) + me * 512
    pos = col.astype(F32) / (256 * 512.0)

    def project(u):
        rows = xs[unit_of(core0, u)[0]].reshape(256, 512)
        proj = jnp.dot(rows, wv[...], preferred_element_type=F32)
        inv = 1.0 / jnp.sqrt(jnp.sum(proj * proj, axis=1, keepdims=True))
        qown[u] = (proj * inv).astype(BF16)

    def to_sib(u):
        return rcopy(qown.at[u], qsib.at[u], q_send.at[u], q_recv.at[u], sib)

    def score(q, bases):
        n = 256 * len(bases)
        lane = lax.broadcasted_iota(jnp.int32, (n, 128), 1)
        d = lax.dot_general(q, gv[...], (((1,), (1,)), ((), ())), preferred_element_type=F32)
        dm = jnp.max(d, axis=1, keepdims=True)
        ev = jnp.exp2((d - dm) * k2)
        zs = jnp.sum(ev, axis=1, keepdims=True)
        rs = jnp.sum(ev * pos, axis=1, keepdims=True)
        cols = jnp.where(lane == 0, dm, jnp.where(lane == 1, zs, rs))
        for i, base in enumerate(bases):
            for b in range(2):
                rows = slice(i * 256 + b * 128, i * 256 + b * 128 + 128)
                e_ref[base + b] = ev[rows]
                stat[base + b] = cols[rows].T[:8]

    def base_own(u):
        return unit_of(core0, u)[1]

    def base_sib(u):
        return unit_of(core1, u)[1]

    def score_both(uo, us):
        score(jnp.concatenate([qown[uo], qsib[us]], axis=0), [base_own(uo), base_sib(us)])

    def send_group(gq):
        @pl.when(gq != pi)
        def _():
            rcopy(stat.at[gq], part.at[pi], s1_send.at[gq], s1_recv.at[pi], z * 32 + gq).start()

        @pl.when(gq == pi)
        def _():
            part[pi] = stat[pi]

    def send_own(u, carry):
        send_group(base_own(u))
        send_group(base_own(u) + 1)
        return carry

    def send_sib(u, carry):
        send_group(base_sib(u))
        send_group(base_sib(u) + 1)
        return carry

    project(0)
    to_sib(0).start()
    events(1)
    project(1)
    to_sib(1).start()
    score(qown[0], [base_own(0)])

    def body(k, carry):
        events(k)
        with scope("sibwait"):
            to_sib(k - 2).wait_recv()
        with scope("compute"):
            score_both(k - 1, k - 2)
            project(k)
        to_sib(k).start()

        @pl.when(k >= 5)
        def _():
            lax.fori_loop(jnp.where(k == 5, 0, k - 2), k - 1, send_own, 0)
            lax.fori_loop(jnp.where(k == 5, 0, k - 3), k - 2, send_sib, 0)

        return carry

    lax.fori_loop(2, 8, body, 0)
    with scope("tail6"):
        to_sib(6).wait_recv()
        score_both(7, 6)
    lax.fori_loop(6, 8, send_own, 0)
    lax.fori_loop(5, 7, send_sib, 0)
    with scope("tail7"):
        to_sib(7).wait_recv()
        score(qsib[7], [base_sib(7)])
    send_sib(7, 0)

    def wait_part(k, carry):
        @pl.when(k != pi)
        def _():
            rcopy(part.at[k], part.at[k], s1_send.at[0], s1_recv.at[k], sib).wait_recv()
        return carry

    with scope("s1wait"):
        lax.fori_loop(0, 32, wait_part, 0)

    def merge(ref):
        ms = ref[:, 0, :]
        m = jnp.max(ms, axis=0, keepdims=True)
        wgt = jnp.exp2((ms - m) * k2)
        return m, jnp.sum(wgt * ref[:, 1, :], axis=0, keepdims=True), jnp.sum(wgt * ref[:, 2, :], axis=0, keepdims=True)

    sub = lax.broadcasted_iota(jnp.int32, (8, 128), 0)

    def tile(a, b, d):
        return jnp.where(sub == 0, a, jnp.where(sub == 1, b, d))

    zpart[z] = tile(*merge(part))
    for d in range(1, NZ):
        rcopy(zpart.at[z], zpart.at[z], s2_send.at[d - 1], s2_recv.at[NZ - d - 1], z_peers[d - 1]).start()
    with scope("s2wait"):
        for d in range(1, NZ):
            zz = lax.rem(z + d, NZ)
            rcopy(zpart.at[zz], zpart.at[zz], s2_send.at[d - 1], s2_recv.at[d - 1], sib).wait_recv()
    m, zs, rs = merge(zpart)
    done[pi] = tile(m, 1.0 / zs, rs / zs)

    def send_done(k, carry):
        p = lax.rem(pi + k, 32)
        rcopy(done.at[pi], done.at[pi], s3_send.at[k - 1], s3_recv.at[31 - k], z * 32 + p).start()
        return carry

    with scope("s3send"):
        lax.fori_loop(1, 32, send_done, 0)

    def wait_done(k, carry):
        p = lax.rem(pi + k, 32)
        rcopy(done.at[p], done.at[p], s3_send.at[k - 1], s3_recv.at[k - 1], sib).wait_recv()
        return carry

    with scope("s3wait"):
        lax.fori_loop(1, 32, wait_done, 0)
    fac_ref[...] = jnp.exp2((stat[:, 0, :] - done[:, 0, :]) * k2) * done[:, 1, :]
    rank_ref[...] = done[:, 2, :]

    def sent(ref, sem):
        rcopy(ref, ref, sem, sem, sib).wait_send()

    with scope("drain"):
        small = xs.at[0, 0, 0]
        line = xs.at[0, 0]

        def drain_lines(k, carry):
            sent(line, r_send.at[k])
            sent(line, l_send.at[k])
            return carry

        lax.fori_loop(0, 8, drain_lines, 0)

        @pl.when(core0)
        def _():
            for d in range(3):
                sent(small, a_send.at[d])
                sent(line, y_send.at[d])
            for k in range(8, 12):
                sent(line, r_send.at[k])
                sent(line, l_send.at[k])
            for k in range(12, 14):
                sent(line, r_send.at[k])
                sent(line, l_send.at[k + 2])

        @pl.when(core1)
        def _():
            for d in range(7):
                sent(small, a_send.at[d])
            for d in range(6):
                sent(line, y_send.at[d])
            for k in range(8, 12):
                sent(line, r_send.at[k])
                sent(line, l_send.at[k])

        for d in range(1, NZ):
            sent(zpart.at[0], s2_send.at[d - 1])

        def drain_q(k, carry):
            sent(qown.at[0], q_send.at[k])
            return carry

        lax.fori_loop(0, 8, drain_q, 0)

        def drain(k, carry):
            @pl.when(k != pi)
            def _():
                sent(stat.at[0], s1_send.at[k])

            @pl.when(k < 31)
            def _():
                sent(stat.at[0], s3_send.at[k])
            return carry

        lax.fori_loop(0, 32, drain, 0)


def normalise_kernel(e_ref, fac_ref, rank_ref, p_hbm, r_ref, buf, nat, sem):
    def scaled(gq):
        f = jnp.broadcast_to(fac_ref[pl.ds(gq, 1), :], (128, 128)).T
        ev = e_ref[gq]
        return jnp.concatenate([ev[:, b * 128:(b + 1) * 128] * f for b in range(4)], axis=1).astype(BF16)

    def out_a(u):
        return pltpu.make_async_copy(buf.at[u], p_hbm.at[u, :, :, 0], sem.at[u])

    def out_b(u):
        return pltpu.make_async_copy(buf.at[8 + u], p_hbm.at[pl.ds(lax.rem(u, 2) * 4, 4), :, u // 2, 1], sem.at[8 + u])

    def body(u, carry):
        for part, base in ((u, 2 * u), (8 + u, 16 + 2 * u)):
            for b in range(2):
                buf[part, 2 * b:2 * b + 2] = scaled(base + b).reshape(2, 4, 16, 512)
        out_a(u).start()
        out_b(u).start()
        return carry

    lax.fori_loop(0, 8, body, 0)

    lane = lax.broadcasted_iota(jnp.int32, (32, 128), 1)
    sub = lax.broadcasted_iota(jnp.int32, (32, 128), 0)
    for n in range(32):
        nat[0, n:n + 1] = rank_ref[pl.ds(n // 2, 1), :]
        for xx in range(NX):
            nat[1 + xx, n:n + 1] = rank_ref[pl.ds(16 + xx * 4 + n // 8, 1), :]
    a = nat[0]
    a = jnp.where(lax.rem(sub, 2) == 0, a, pltpu.roll(a, 64, 1))
    out = jnp.where(lane < 16, a, 0.0)
    for xx in range(1, NX):
        out = jnp.where(lane // 16 == 2 * xx, pltpu.roll(a, 16 * xx, 1), out)
    for xx in range(NX):
        b = nat[1 + xx]
        for s in range(8):
            shift = (xx * 32 + 16 - s * 16) % 128
            r = pltpu.roll(b, shift, 1) if shift else b
            out = jnp.where(jnp.logical_and(lax.rem(sub, 8) == s, lane // 16 == 2 * xx + 1), r, out)
    r_ref[...] = out

    def flush(u, carry):
        out_a(u).wait()
        out_b(u).wait()
        return carry

    lax.fori_loop(0, 8, flush, 0)


def solution(mesh):
    D = pltpu.SemaphoreType.DMA
    VM = pltpu.VMEM

    def per_device(text_states, text_proj, gallery, logit_scale):
        e, fac, rank = pl.pallas_call(
            gather_score_kernel,
            out_shape=(VM((32, 128, 512), F32), VM((32, 128), F32), VM((32, 128), F32)),
            in_specs=[pl.BlockSpec(memory_space=pl.ANY)] * 3 + [pl.BlockSpec(memory_space=VM)],
            out_specs=(pl.BlockSpec(memory_space=VM),) * 3,
            scratch_shapes=[
                VM((8, 4, 4, 16, 512), BF16), VM((512, 1024), BF16), VM((512, 1024), BF16),
                VM((8, 256, 1024), BF16), VM((8, 256, 1024), BF16),
                VM((32, 8, 128), F32), VM((32, 8, 128), F32), VM((NZ, 8, 128), F32), VM((32, 8, 128), F32),
                D((3,)), D((7,)), D((7,)), D((6,)), D((6,)),
                D((16,)), D((16,)), D((16,)), D((16,)), D((8,)), D((8,)),
                D((32,)), D((32,)), D((7,)), D((7,)), D((31,)), D((31,)),
            ],
            compiler_params=pltpu.CompilerParams(collective_id=0, has_side_effects=True,
                                                 vmem_limit_bytes=48 * 1024 * 1024),
        )(text_states, text_proj, gallery, logit_scale.reshape(1, 1))
        prob, rank = pl.pallas_call(
            normalise_kernel,
            out_shape=(jax.ShapeDtypeStruct((NZ, NY, NX, NC, 16, 512), BF16), jax.ShapeDtypeStruct((32, 128), F32)),
            in_specs=[pl.BlockSpec(memory_space=VM)] * 3,
            out_specs=(pl.BlockSpec(memory_space=pl.ANY), pl.BlockSpec(memory_space=VM)),
            scratch_shapes=[VM((16, 4, 4, 16, 512), BF16), VM((5, 32, 128), F32), D((16,))],
            compiler_params=pltpu.CompilerParams(vmem_limit_bytes=24 * 1024 * 1024),
        )(e, fac, rank)
        return prob.reshape(4096, 512), rank.reshape(4096)

    return jax.shard_map(per_device, mesh=mesh,
                         in_specs=(P("ga", None), P(None, None), P("ga", None), P(None)),
                         out_specs=(P(None, "ga"), P(None)), check_vma=False)
```

time: 391 us -> 59.6 us (0.15)
  blocking collectives: 222 us -> 0 us
  waiting for transfers between devices: 124 us -> 0 us
  Pallas kernels: 0 us -> 58.2 us
  between operations: 14.7 us -> 1.28 us
  matrix products: 11.8 us -> 0 us
  other arithmetic: 11.3 us -> 0 us
  local copies, waits for them, and re-layouts: 6.42 us -> 0 us
    psum x2 -> x0, blocking collectives: 148 us -> none  [the longest x1 73.9 us: per_device(): glob_sum = lax.psum(jnp.sum(exp_vals, axis=1), 'ga')]
    all_gather x1 -> x0, waiting for transfers between devices: 124 us -> none  [per_device(): all_queries = lax.all_gather(query_emb, 'ga', axis=0, tiled=True)]
    pmax x1 -> x0, blocking collectives: 74.5 us -> none  [per_device(): glob_max = lax.pmax(jnp.max(scores, axis=1), 'ga')]
    pallas_call x0 -> x2, Pallas kernels: none -> 58.2 us  [the longest x1 55.4 us: per_device(): pl.pallas_call(gather_score_kernel, out_shape=(VM((32, 128, 512), F32), V...]
    dot_general x2 -> x0, matrix products: 11.8 us -> none  [the longest x1 10.1 us: per_device(): lax.dot_general(all_queries, gallery, (((1,), (1,)), ((), ())), preferred...]
    reduce_sum x2 -> x0, other arithmetic: 10.6 us -> none  [the longest x1 5.86 us: per_device(): exp_rank = lax.psum(jnp.sum(prob_vals * positions, axis=1), 'ga')]
    unnamed x3 -> x0, local copies, waits for them, and re-layouts: 6.41 us -> none
  transfers between devices with their start and end apart: 1 -> 0, of which waited for: 1 -> 0; matrix products, arithmetic and copies ran while one was open for 0% -> 0% of each run, Pallas kernels for 0% -> 0%
where the time goes in v2:
time: 59.6 us; the launch traced here: 59.5 us
  Pallas kernels  58.2 us (98%)
  between operations  1.28 us (2%)
    pallas_call x1, Pallas kernels, per_device(): pl.pallas_call(gather_score_kernel, out_shape=(VM((32, 128, 512), F32), V...  55.4 us
    pallas_call x1, Pallas kernels, per_device(): pl.pallas_call(normalise_kernel, out_shape=(jax.ShapeDtypeStruct((NZ, NY,...  2.88 us

profile of v2, /device:TPU:1, one launch (start us, length us, event | category | flops | bytes accessed | tf_op | source)
XLA Modules:
  0.0 59.5 jit_solution(11613487504775876383)
XLA Ops:
  1.3 55.4 %shard_map.59 = (f32[32,128,512]{2,1,0:T(8,128)S(1)}, f32[32,128]{1,0:T(8,128)S(1)}, f32[32,128]{1,0:T(8,128)S(1)}) custom-call(bf16[16,512]{1,0:T(8,128)(2,1)} %x_hbm.1, bf16[512,1024]{1,0:T(8,128)(2,1)} %w_hbm.1, bf16[512,1024]{1,0:T(8,128)(2,1)} %g_hbm.1, f32[1,1]{1,0:T(1,128)} %bitcast.3.t_ref), custom_call_target="tpu_custom_call" | custom-call | tf_op jit(solution)/shard_map/pallas_call | solution.py:442
  56.6 2.9 %shard_map.60 = (bf16[8,4,4,2,16,512]{5,4,3,2,1,0:T(8,128)(2,1)}, f32[32,128]{1,0:T(8,128)}) custom-call(f32[32,128,512]{2,1,0:T(8,128)S(1)} %get-tuple-element.7.e_ref, f32[32,128]{1,0:T(8,128)S(1)} %get-tuple-element.8.fac_ref, f32[32,128]{1,0:T(8,128)S(1)} %get-tuple-element.9.rank_ref), custom_call_target="tpu_custom_call" | custom-call | tf_op jit(solution)/shard_map/pallas_call | solution.py:458

commit v3 on v0

v3 whole, which is shorter than its diff:
```python
import jax
import jax.numpy as jnp
from jax import lax
from jax.experimental import pallas as pl
from jax.experimental.pallas import tpu as pltpu
from jax.sharding import PartitionSpec as P

MESH = pl.DeviceIdType.MESH
NX, NY, NZ, NC = 4, 4, 8, 2
F32, BF16 = jnp.float32, jnp.bfloat16
LOG2E = 1.4426950408889634
F32_MAX = 3.4028235e38
scope = jax.named_scope


def rcopy(src, dst, ss, rs, p):
    return pltpu.make_async_remote_copy(src_ref=src, dst_ref=dst, send_sem=ss, recv_sem=rs,
                                        device_id=(p,), device_id_type=MESH)


def gather_score_kernel(x_hbm, w_hbm, g_hbm, t_ref,
                        e_ref, fac_ref, rank_ref,
                        xs, wv, gv, qown, qsib, stat, part, zpart, done,
                        in_sem, a_sem, y_send, y_recv, r_send, r_recv, l_send, l_recv,
                        q_send, q_recv, s_send, s_recv):
    me = lax.axis_index("ga")
    c = lax.rem(me, NC)
    x = lax.rem(me // 2, NX)
    y = lax.rem(me // 8, NY)
    z = me // 32
    pi = lax.rem(me, 32)
    core0 = c == 0
    ml = jnp.where(core0, y, x)
    ll = jnp.where(core0, x, y)

    def dev(zz, yy, xx, cc):
        return ((zz * NY + yy) * NX + xx) * NC + cc

    def dev_lm(zz, lc, mc):
        return dev(zz, jnp.where(core0, mc, lc), jnp.where(core0, lc, mc), c)

    def column(lc, mc):
        return lc * 4 + mc

    mine = column(ll, ml)
    own = xs.at[mine, z]
    load_x = pltpu.make_async_copy(x_hbm, own, in_sem.at[0])
    load_w = pltpu.make_async_copy(w_hbm, wv, in_sem.at[1])
    load_g = pltpu.make_async_copy(g_hbm, gv, in_sem.at[2])
    load_x.start()
    load_w.start()
    load_g.start()

    sib = dev(z, y, x, 1 - c)
    z_peers = [dev(lax.rem(z + d, NZ), y, x, c) for d in range(1, NZ)]
    m_peers = [dev_lm(z, ll, lax.rem(ml + d, 4)) for d in range(1, 4)]
    right = dev_lm(z, lax.rem(ll + 1, 4), ml)
    left = dev_lm(z, lax.rem(ll + 3, 4), ml)

    barrier = pltpu.get_barrier_semaphore()
    with scope("barrier"):
        peers = [sib, right, left] + m_peers + z_peers
        for p in peers:
            pl.semaphore_signal(barrier, inc=1, device_id=(p,), device_id_type=MESH)
        pl.semaphore_wait(barrier, len(peers))
        load_x.wait()

    for d in range(1, NZ):
        rcopy(own, own, a_sem.at[0], a_sem.at[1], z_peers[d - 1]).start()
    with scope("first"):
        rcopy(xs.at[0, 0:7], xs.at[0, 0:7], a_sem.at[0], a_sem.at[1], sib).wait_recv()

    def col(lc, j):
        off = jnp.where(j == 0, 0, jnp.where(j == 1, 1, jnp.where(j == 2, 3, 2)))
        return xs.at[column(lc, lax.rem(ml + off, 4))]

    def to_right(lc, j, e):
        return rcopy(col(lc, j), col(lc, j), r_send.at[0], r_recv.at[e], right)

    def to_left(lc, j, e):
        return rcopy(col(lc, j), col(lc, j), l_send.at[0], l_recv.at[e], left)

    lp, lm, lf = lax.rem(ll + 1, 4), lax.rem(ll + 3, 4), lax.rem(ll + 2, 4)

    for d in range(1, 4):
        rcopy(xs.at[mine], xs.at[mine], y_send.at[0], y_recv.at[3 - d], m_peers[d - 1]).start()
    to_right(ll, 0, 0).start()
    to_left(ll, 0, 0).start()

    def mid(j, off):
        with scope("second"):
            rcopy(col(ll, j), col(ll, j), y_send.at[0], y_recv.at[off - 1], sib).wait_recv()
        to_right(ll, j, j).start()
        to_left(ll, j, j).start()

    def event(e):
        to_right(lm, e, e).wait_recv()

        @pl.when(e < 2)
        def _():
            to_right(lm, e, 4 + e).start()

        to_left(lp, e, e).wait_recv()

        @pl.when(e >= 2)
        def _():
            to_left(lp, e, 2 + e).start()

    def unit_of(lc, mc, u):
        far = u >= 6
        odd = lax.rem(u, 2) == 1
        dl = jnp.where(u < 2, 0, jnp.where(far, 2, jnp.where(odd, 1, 3)))
        second = jnp.logical_or(jnp.logical_or(u == 1, u == 7), jnp.logical_or(u == 4, u == 5))
        m1 = lax.rem(mc + jnp.where(second, 3, 0), 4)
        m2 = lax.rem(mc + jnp.where(second, 2, 1), 4)
        return lax.rem(lc + dl, 4), m1, m2

    load_w.wait()
    load_g.wait()
    k2 = jnp.minimum(jnp.exp(t_ref[...]) * LOG2E, F32_MAX)
    place = lax.broadcasted_iota(jnp.int32, (1, 512), 1) + me * 512
    pos = place.astype(F32) / (256 * 512.0)

    def project(u):
        lc, m1, m2 = unit_of(ll, ml, u)
        rows = jnp.concatenate([xs[column(lc, m1)].reshape(128, 512), xs[column(lc, m2)].reshape(128, 512)], axis=0)
        proj = jnp.dot(rows, wv[...], preferred_element_type=F32)
        inv = 1.0 / jnp.sqrt(jnp.sum(proj * proj, axis=1, keepdims=True))
        qown[u] = (proj * inv).astype(BF16)

    def to_sib(u):
        return rcopy(qown.at[u], qsib.at[u], q_send.at[0], q_recv.at[u], sib)

    def score(q, groups):
        n = 128 * len(groups)
        lane = lax.broadcasted_iota(jnp.int32, (n, 128), 1)
        d = lax.dot_general(q, gv[...], (((1,), (1,)), ((), ())), preferred_element_type=F32)
        dm = jnp.max(d, axis=1, keepdims=True)
        ev = jnp.exp2((d - dm) * k2)
        zs = jnp.sum(ev, axis=1, keepdims=True)
        rs = jnp.sum(ev * pos, axis=1, keepdims=True)
        cols = jnp.where(lane == 0, dm, jnp.where(lane == 1, zs, rs))
        for i, gq in enumerate(groups):
            rows = slice(i * 128, i * 128 + 128)
            e_ref[gq] = ev[rows]
            stat[gq] = cols[rows].T[:8]

    def groups_own(u):
        lc, m1, m2 = unit_of(ll, ml, u)
        return [jnp.where(core0, m * 8 + lc * 2, lc * 8 + m * 2 + 1) for m in (m1, m2)]

    def groups_sib(u):
        lc, m1, m2 = unit_of(ml, ll, u)
        return [jnp.where(core0, lc * 8 + m * 2 + 1, m * 8 + lc * 2) for m in (m1, m2)]

    def score_both(uo, us):
        score(jnp.concatenate([qown[uo], qsib[us]], axis=0), groups_own(uo) + groups_sib(us))

    def send_group(gq):
        @pl.when(gq != pi)
        def _():
            rcopy(stat.at[gq], part.at[pi], s_send.at[0], s_recv.at[0], z * 32 + gq).start()

        @pl.when(gq == pi)
        def _():
            part[pi] = stat[pi]

    def send_own(u, carry):
        for gq in groups_own(u):
            send_group(gq)
        return carry

    def send_sib(u, carry):
        for gq in groups_sib(u):
            send_group(gq)
        return carry

    mid(1, 1)
    mid(2, 3)
    project(0)
    to_sib(0).start()
    mid(3, 2)
    with scope("event0"):
        event(0)
    project(1)
    to_sib(1).start()
    score(qown[0], groups_own(0))

    def body(k, carry):
        with scope("events"):
            @pl.when(k <= 4)
            def _():
                event(k - 1)

            @pl.when(k == 6)
            def _():
                for e in range(4, 6):
                    to_right(lf, e - 4, e).wait_recv()

            @pl.when(k == 7)
            def _():
                for e in range(4, 6):
                    to_left(lf, e - 2, e).wait_recv()

        with scope("sibwait"):
            to_sib(k - 2).wait_recv()
        with scope("compute"):
            score_both(k - 1, k - 2)
            project(k)
        to_sib(k).start()

        @pl.when(k >= 5)
        def _():
            lax.fori_loop(jnp.where(k == 5, 0, k - 2), k - 1, send_own, 0)
            lax.fori_loop(jnp.where(k == 5, 0, k - 3), k - 2, send_sib, 0)

        return carry

    lax.fori_loop(2, 8, body, 0)
    with scope("tail6"):
        to_sib(6).wait_recv()
        score_both(7, 6)
    lax.fori_loop(6, 8, send_own, 0)
    lax.fori_loop(5, 7, send_sib, 0)
    with scope("tail7"):
        to_sib(7).wait_recv()
        score(qsib[7], groups_sib(7))
    send_sib(7, 0)

    with scope("s1wait"):
        rcopy(part.at[0:31], part.at[0:31], s_send.at[0], s_recv.at[0], sib).wait_recv()

    def merge(ref):
        ms = ref[:, 0, :]
        m = jnp.max(ms, axis=0, keepdims=True)
        wgt = jnp.exp2((ms - m) * k2)
        return m, jnp.sum(wgt * ref[:, 1, :], axis=0, keepdims=True), jnp.sum(wgt * ref[:, 2, :], axis=0, keepdims=True)

    sub = lax.broadcasted_iota(jnp.int32, (8, 128), 0)

    def tile(a, b, d):
        return jnp.where(sub == 0, a, jnp.where(sub == 1, b, d))

    zpart[z] = tile(*merge(part))
    for d in range(1, NZ):
        rcopy(zpart.at[z], zpart.at[z], s_send.at[1], s_recv.at[1], z_peers[d - 1]).start()
    with scope("s2wait"):
        rcopy(zpart.at[0:7], zpart.at[0:7], s_send.at[1], s_recv.at[1], sib).wait_recv()
    m, zs, rs = merge(zpart)
    done[pi] = tile(m, 1.0 / zs, rs / zs)

    def send_done(k, carry):
        p = lax.rem(pi + k, 32)
        rcopy(done.at[pi], done.at[pi], s_send.at[2], s_recv.at[2], z * 32 + p).start()
        return carry

    with scope("s3send"):
        lax.fori_loop(1, 32, send_done, 0)

    with scope("s3wait"):
        rcopy(done.at[0:31], done.at[0:31], s_send.at[2], s_recv.at[2], sib).wait_recv()
    fac_ref[...] = jnp.exp2((stat[:, 0, :] - done[:, 0, :]) * k2) * done[:, 1, :]
    rank_ref[...] = done[:, 2, :]

    def sent(ref, sem):
        rcopy(ref, ref, sem, sem, sib).wait_send()

    with scope("drain"):
        sent(xs.at[0, 0:7], a_sem.at[0])
        sent(xs.at[0:3], y_send.at[0])
        sent(xs.at[0:6], r_send.at[0])
        sent(xs.at[0:6], l_send.at[0])
        sent(qown, q_send.at[0])
        sent(part.at[0:31], s_send.at[0])
        sent(zpart.at[0:7], s_send.at[1])
        sent(done.at[0:31], s_send.at[2])


def normalise_kernel(e_ref, fac_ref, rank_ref, p_hbm, r_ref, buf, sem):
    def out(gq):
        return pltpu.make_async_copy(buf.at[gq], p_hbm.at[:, gq], sem.at[gq])

    def body(gq, carry):
        f = jnp.broadcast_to(fac_ref[pl.ds(gq, 1), :], (128, 128)).T
        ev = e_ref[gq]
        p = jnp.concatenate([ev[:, b * 128:(b + 1) * 128] * f for b in range(4)], axis=1)
        buf[gq] = p.astype(BF16).reshape(8, 16, 512)
        out(gq).start()
        return carry

    lax.fori_loop(0, 32, body, 0)

    lane = lax.broadcasted_iota(jnp.int32, (8, 128), 1) // 16
    sub = lax.broadcasted_iota(jnp.int32, (8, 128), 0)
    for yy in range(NY):
        r = rank_ref[yy * 8:yy * 8 + 8]
        nat = r
        for d in range(1, 8):
            moved = pltpu.roll(pltpu.roll(r, 16 * d, 1), 8 - d, 0)
            nat = jnp.where(lax.rem(lane - sub + 8, 8) == d, moved, nat)
        r_ref[pl.ds(yy, 8, stride=4), :] = nat

    def flush(gq, carry):
        out(gq).wait()
        return carry

    lax.fori_loop(0, 32, flush, 0)


def solution(mesh):
    D = pltpu.SemaphoreType.DMA
    VM = pltpu.VMEM

    def per_device(text_states, text_proj, gallery, logit_scale):
        e, fac, rank = pl.pallas_call(
            gather_score_kernel,
            out_shape=(VM((32, 128, 512), F32), VM((32, 128), F32), VM((32, 128), F32)),
            in_specs=[pl.BlockSpec(memory_space=pl.ANY)] * 3 + [pl.BlockSpec(memory_space=VM)],
            out_specs=(pl.BlockSpec(memory_space=VM),) * 3,
            scratch_shapes=[
                VM((16, NZ, 16, 512), BF16), VM((512, 1024), BF16), VM((512, 1024), BF16),
                VM((8, 256, 1024), BF16), VM((8, 256, 1024), BF16),
                VM((32, 8, 128), F32), VM((32, 8, 128), F32), VM((NZ, 8, 128), F32), VM((32, 8, 128), F32),
                D((3,)), D((2,)), D((1,)), D((3,)), D((1,)), D((6,)), D((1,)), D((6,)),
                D((1,)), D((8,)), D((3,)), D((3,)),
            ],
            compiler_params=pltpu.CompilerParams(collective_id=0, has_side_effects=True,
                                                 vmem_limit_bytes=48 * 1024 * 1024),
        )(text_states, text_proj, gallery, logit_scale.reshape(1, 1))
        prob, rank = pl.pallas_call(
            normalise_kernel,
            out_shape=(jax.ShapeDtypeStruct((NZ, 32, 16, 512), BF16), jax.ShapeDtypeStruct((32, 128), F32)),
            in_specs=[pl.BlockSpec(memory_space=VM)] * 3,
            out_specs=(pl.BlockSpec(memory_space=pl.ANY), pl.BlockSpec(memory_space=VM)),
            scratch_shapes=[VM((32, NZ, 16, 512), BF16), D((32,))],
            compiler_params=pltpu.CompilerParams(vmem_limit_bytes=24 * 1024 * 1024),
        )(e, fac, rank)
        return prob.reshape(4096, 512), rank.reshape(4096)

    return jax.shard_map(per_device, mesh=mesh,
                         in_specs=(P("ga", None), P(None, None), P("ga", None), P(None)),
                         out_specs=(P(None, "ga"), P(None)), check_vma=False)
```

time: 391 us -> 58.9 us (0.15)
  blocking collectives: 222 us -> 0 us
  waiting for transfers between devices: 124 us -> 0 us
  Pallas kernels: 0 us -> 57.5 us
  between operations: 14.7 us -> 1.28 us
  matrix products: 11.8 us -> 0 us
  other arithmetic: 11.3 us -> 0 us
  local copies, waits for them, and re-layouts: 6.42 us -> 0 us
    psum x2 -> x0, blocking collectives: 148 us -> none  [the longest x1 73.9 us: per_device(): glob_sum = lax.psum(jnp.sum(exp_vals, axis=1), 'ga')]
    all_gather x1 -> x0, waiting for transfers between devices: 124 us -> none  [per_device(): all_queries = lax.all_gather(query_emb, 'ga', axis=0, tiled=True)]
    pmax x1 -> x0, blocking collectives: 74.5 us -> none  [per_device(): glob_max = lax.pmax(jnp.max(scores, axis=1), 'ga')]
    pallas_call x0 -> x2, Pallas kernels: none -> 57.5 us  [the longest x1 52.6 us: per_device(): pl.pallas_call(gather_score_kernel, out_shape=(VM((32, 128, 512), F32), V...]
    dot_general x2 -> x0, matrix products: 11.8 us -> none  [the longest x1 10.1 us: per_device(): lax.dot_general(all_queries, gallery, (((1,), (1,)), ((), ())), preferred...]
    reduce_sum x2 -> x0, other arithmetic: 10.6 us -> none  [the longest x1 5.86 us: per_device(): exp_rank = lax.psum(jnp.sum(prob_vals * positions, axis=1), 'ga')]
    unnamed x3 -> x0, local copies, waits for them, and re-layouts: 6.41 us -> none
  transfers between devices with their start and end apart: 1 -> 0, of which waited for: 1 -> 0; matrix products, arithmetic and copies ran while one was open for 0% -> 0% of each run, Pallas kernels for 0% -> 0%
where the time goes in v3:
time: 58.9 us; the launch traced here: 58.8 us
  Pallas kernels  57.5 us (98%)
  between operations  1.28 us (2%)
    pallas_call x1, Pallas kernels, per_device(): pl.pallas_call(gather_score_kernel, out_shape=(VM((32, 128, 512), F32), V...  52.6 us
    pallas_call x1, Pallas kernels, per_device(): pl.pallas_call(normalise_kernel, out_shape=(jax.ShapeDtypeStruct((NZ, 32,...  4.85 us

profile of v3, /device:TPU:1, one launch (start us, length us, event | category | flops | bytes accessed | tf_op | source)
XLA Modules:
  0.0 58.8 jit_solution(12104261829779972969)
XLA Ops:
  1.3 52.6 %shard_map.59 = (f32[32,128,512]{2,1,0:T(8,128)S(1)}, f32[32,128]{1,0:T(8,128)S(1)}, f32[32,128]{1,0:T(8,128)S(1)}) custom-call(bf16[16,512]{1,0:T(8,128)(2,1)} %x_hbm.1, bf16[512,1024]{1,0:T(8,128)(2,1)} %w_hbm.1, bf16[512,1024]{1,0:T(8,128)(2,1)} %g_hbm.1, f32[1,1]{1,0:T(1,128)} %bitcast.3.t_ref), custom_call_target="tpu_custom_call" | custom-call | tf_op jit(solution)/shard_map/pallas_call | solution.py:315
  53.9 4.8 %shard_map.60 = (bf16[8,32,16,512]{3,2,1,0:T(8,128)(2,1)}, f32[32,128]{1,0:T(8,128)}) custom-call(f32[32,128,512]{2,1,0:T(8,128)S(1)} %get-tuple-element.7.e_ref, f32[32,128]{1,0:T(8,128)S(1)} %get-tuple-element.8.fac_ref, f32[32,128]{1,0:T(8,128)S(1)} %get-tuple-element.9.rank_ref), custom_call_target="tpu_custom_call" | custom-call | tf_op jit(solution)/shard_map/pallas_call | solution.py:330

commit v4 on v3

--- a/solution.py
+++ b/solution.py
@@ -20,7 +20,7 @@
 
 def gather_score_kernel(x_hbm, w_hbm, g_hbm, t_ref,
                         e_ref, fac_ref, rank_ref,
-                        xs, wv, gv, qown, qsib, stat, part, zpart, done,
+                        xs, wv, gv, qown, qsib, da, db, stat, part, zpart, done,
                         in_sem, a_sem, y_send, y_recv, r_send, r_recv, l_send, l_recv,
                         q_send, q_recv, s_send, s_recv):
     me = lax.axis_index("ga")
@@ -117,7 +117,7 @@
 
     load_w.wait()
     load_g.wait()
-    k2 = jnp.minimum(jnp.exp(t_ref[...]) * LOG2E, F32_MAX)
+    k2 = jnp.minimum(jnp.exp(jnp.full((1, 1), t_ref[0], F32)) * LOG2E, F32_MAX)
     place = lax.broadcasted_iota(jnp.int32, (1, 512), 1) + me * 512
     pos = place.astype(F32) / (256 * 512.0)
 
@@ -131,10 +131,14 @@
     def to_sib(u):
         return rcopy(qown.at[u], qsib.at[u], q_send.at[0], q_recv.at[u], sib)
 
-    def score(q, groups):
+    def dots(buf, qs):
+        q = qs[0] if len(qs) == 1 else jnp.concatenate(qs, axis=0)
+        buf[0:256 * len(qs)] = lax.dot_general(q, gv[...], (((1,), (1,)), ((), ())), preferred_element_type=F32)
+
+    def soften(buf, groups):
         n = 128 * len(groups)
         lane = lax.broadcasted_iota(jnp.int32, (n, 128), 1)
-        d = lax.dot_general(q, gv[...], (((1,), (1,)), ((), ())), preferred_element_type=F32)
+        d = buf[0:n]
         dm = jnp.max(d, axis=1, keepdims=True)
         ev = jnp.exp2((d - dm) * k2)
         zs = jnp.sum(ev, axis=1, keepdims=True)
@@ -153,8 +157,8 @@
         lc, m1, m2 = unit_of(ml, ll, u)
         return [jnp.where(core0, lc * 8 + m * 2 + 1, m * 8 + lc * 2) for m in (m1, m2)]
 
-    def score_both(uo, us):
-        score(jnp.concatenate([qown[uo], qsib[us]], axis=0), groups_own(uo) + groups_sib(us))
+    def groups_both(uo, us):
+        return groups_own(uo) + groups_sib(us)
 
     def send_group(gq):
         @pl.when(gq != pi)
@@ -183,10 +187,10 @@
     with scope("event0"):
         event(0)
     project(1)
+    dots(da, [qown[0]])
     to_sib(1).start()
-    score(qown[0], groups_own(0))
-
-    def body(k, carry):
+
+    def step(k, now, before, first):
         with scope("events"):
             @pl.when(k <= 4)
             def _():
@@ -205,26 +209,47 @@
         with scope("sibwait"):
             to_sib(k - 2).wait_recv()
         with scope("compute"):
-            score_both(k - 1, k - 2)
+            soften(before, groups_own(0) if first else groups_both(k - 2, k - 3))
             project(k)
+            dots(now, [qown[k - 1], qsib[k - 2]])
         to_sib(k).start()
 
-        @pl.when(k >= 5)
-        def _():
-            lax.fori_loop(jnp.where(k == 5, 0, k - 2), k - 1, send_own, 0)
-            lax.fori_loop(jnp.where(k == 5, 0, k - 3), k - 2, send_sib, 0)
-
-        return carry
-
-    lax.fori_loop(2, 8, body, 0)
+    step(2, db, da, True)
+    step(3, da, db, False)
+
+    def body(i, carry):
+        k = 2 * i
+        step(k, db, da, False)
+
+        @pl.when(i == 3)
+        def _():
+            lax.fori_loop(0, 4, send_own, 0)
+            lax.fori_loop(0, 3, send_sib, 0)
+
+        step(k + 1, da, db, False)
+
+        @pl.when(i == 3)
+        def _():
+            lax.fori_loop(4, 6, send_own, 0)
+            lax.fori_loop(3, 5, send_sib, 0)
+
+        return carry
+
+    lax.fori_loop(2, 4, body, 0)
     with scope("tail6"):
         to_sib(6).wait_recv()
-        score_both(7, 6)
-    lax.fori_loop(6, 8, send_own, 0)
-    lax.fori_loop(5, 7, send_sib, 0)
+        soften(da, groups_both(6, 5))
+        dots(db, [qown[7], qsib[6]])
+    send_own(6, 0)
+    send_sib(5, 0)
     with scope("tail7"):
         to_sib(7).wait_recv()
-        score(qsib[7], groups_sib(7))
+        soften(db, groups_both(7, 6))
+        dots(da, [qsib[7]])
+    send_own(7, 0)
+    send_sib(6, 0)
+    with scope("tail8"):
+        soften(da, groups_sib(7))
     send_sib(7, 0)
 
     with scope("s1wait"):
@@ -277,18 +302,19 @@
 
 
 def normalise_kernel(e_ref, fac_ref, rank_ref, p_hbm, r_ref, buf, sem):
-    def out(gq):
-        return pltpu.make_async_copy(buf.at[gq], p_hbm.at[:, gq], sem.at[gq])
-
-    def body(gq, carry):
-        f = jnp.broadcast_to(fac_ref[pl.ds(gq, 1), :], (128, 128)).T
-        ev = e_ref[gq]
-        p = jnp.concatenate([ev[:, b * 128:(b + 1) * 128] * f for b in range(4)], axis=1)
-        buf[gq] = p.astype(BF16).reshape(8, 16, 512)
-        out(gq).start()
-        return carry
-
-    lax.fori_loop(0, 32, body, 0)
+    def body(i, carry):
+        for j in range(8):
+            gq = i * 8 + j
+            f = jnp.broadcast_to(fac_ref[pl.ds(gq, 1), :], (128, 128)).T
+            ev = e_ref[gq]
+            p = jnp.concatenate([ev[:, b * 128:(b + 1) * 128] * f for b in range(4)], axis=1)
+            buf[gq] = p.astype(BF16).reshape(8, 16, 512)
+        for j in range(8):
+            gq = i * 8 + j
+            pltpu.make_async_copy(buf.at[gq], p_hbm.at[:, gq], sem.at[i]).start()
+        return carry
+
+    lax.fori_loop(0, 4, body, 0)
 
     lane = lax.broadcasted_iota(jnp.int32, (8, 128), 1) // 16
     sub = lax.broadcasted_iota(jnp.int32, (8, 128), 0)
@@ -300,11 +326,8 @@
             nat = jnp.where(lax.rem(lane - sub + 8, 8) == d, moved, nat)
         r_ref[pl.ds(yy, 8, stride=4), :] = nat
 
-    def flush(gq, carry):
-        out(gq).wait()
-        return carry
-
-    lax.fori_loop(0, 32, flush, 0)
+    for i in range(4):
+        pltpu.make_async_copy(buf.at[0:8], p_hbm.at[:, 0:8], sem.at[i]).wait()
 
 
 def solution(mesh):
@@ -315,24 +338,24 @@
         e, fac, rank = pl.pallas_call(
             gather_score_kernel,
             out_shape=(VM((32, 128, 512), F32), VM((32, 128), F32), VM((32, 128), F32)),
-            in_specs=[pl.BlockSpec(memory_space=pl.ANY)] * 3 + [pl.BlockSpec(memory_space=VM)],
+            in_specs=[pl.BlockSpec(memory_space=pl.ANY)] * 3 + [pl.BlockSpec(memory_space=pltpu.SMEM)],
             out_specs=(pl.BlockSpec(memory_space=VM),) * 3,
             scratch_shapes=[
                 VM((16, NZ, 16, 512), BF16), VM((512, 1024), BF16), VM((512, 1024), BF16),
-                VM((8, 256, 1024), BF16), VM((8, 256, 1024), BF16),
+                VM((8, 256, 1024), BF16), VM((8, 256, 1024), BF16), VM((512, 512), F32), VM((512, 512), F32),
                 VM((32, 8, 128), F32), VM((32, 8, 128), F32), VM((NZ, 8, 128), F32), VM((32, 8, 128), F32),
                 D((3,)), D((2,)), D((1,)), D((3,)), D((1,)), D((6,)), D((1,)), D((6,)),
                 D((1,)), D((8,)), D((3,)), D((3,)),
             ],
             compiler_params=pltpu.CompilerParams(collective_id=0, has_side_effects=True,
                                                  vmem_limit_bytes=48 * 1024 * 1024),
-        )(text_states, text_proj, gallery, logit_scale.reshape(1, 1))
+        )(text_states, text_proj, gallery, logit_scale)
         prob, rank = pl.pallas_call(
             normalise_kernel,
             out_shape=(jax.ShapeDtypeStruct((NZ, 32, 16, 512), BF16), jax.ShapeDtypeStruct((32, 128), F32)),
             in_specs=[pl.BlockSpec(memory_space=VM)] * 3,
             out_specs=(pl.BlockSpec(memory_space=pl.ANY), pl.BlockSpec(memory_space=VM)),
-            scratch_shapes=[VM((32, NZ, 16, 512), BF16), D((32,))],
+            scratch_shapes=[VM((32, NZ, 16, 512), BF16), D((4,))],
             compiler_params=pltpu.CompilerParams(vmem_limit_bytes=24 * 1024 * 1024),
         )(e, fac, rank)
         return prob.reshape(4096, 512), rank.reshape(4096)

time: 58.9 us -> 56.9 us (0.966)
  Pallas kernels: 57.5 us -> 55.5 us
    pallas_call x1, Pallas kernels: 4.85 us -> 2.82 us  [per_device(): pl.pallas_call(normalise_kernel, out_shape=(jax.ShapeDtypeStruct((NZ, 32,...]
where the time goes in v4:
time: 56.9 us; the launch traced here: 56.8 us
  Pallas kernels  55.5 us (98%)
  between operations  1.28 us (2%)
    pallas_call x1, Pallas kernels, per_device(): pl.pallas_call(gather_score_kernel, out_shape=(VM((32, 128, 512), F32), V...  52.7 us
    pallas_call x1, Pallas kernels, per_device(): pl.pallas_call(normalise_kernel, out_shape=(jax.ShapeDtypeStruct((NZ, 32,...  2.82 us

profile of v4, /device:TPU:1, one launch (start us, length us, event | category | flops | bytes accessed | tf_op | source)
XLA Modules:
  0.0 56.8 jit_solution(735684570357582451)
XLA Ops:
  1.3 52.7 %shard_map.59 = (f32[32,128,512]{2,1,0:T(8,128)S(1)}, f32[32,128]{1,0:T(8,128)S(1)}, f32[32,128]{1,0:T(8,128)S(1)}) custom-call(bf16[16,512]{1,0:T(8,128)(2,1)} %x_hbm.1, bf16[512,1024]{1,0:T(8,128)(2,1)} %w_hbm.1, bf16[512,1024]{1,0:T(8,128)(2,1)} %g_hbm.1, f32[1]{0:T(128)S(6)} %copy.6.t_ref), custom_call_target="tpu_custom_call" | custom-call | tf_op jit(solution)/shard_map/pallas_call | solution.py:338
  53.9 2.8 %shard_map.60 = (bf16[8,32,16,512]{3,2,1,0:T(8,128)(2,1)}, f32[32,128]{1,0:T(8,128)}) custom-call(f32[32,128,512]{2,1,0:T(8,128)S(1)} %get-tuple-element.7.e_ref, f32[32,128]{1,0:T(8,128)S(1)} %get-tuple-element.8.fac_ref, f32[32,128]{1,0:T(8,128)S(1)} %get-tuple-element.9.rank_ref), custom_call_target="tpu_custom_call" | custom-call | tf_op jit(solution)/shard_map/pallas_call | solution.py:353

commit v5 on v4

--- a/solution.py
+++ b/solution.py
@@ -53,13 +53,14 @@
 
     sib = dev(z, y, x, 1 - c)
     z_peers = [dev(lax.rem(z + d, NZ), y, x, c) for d in range(1, NZ)]
-    m_peers = [dev_lm(z, ll, lax.rem(ml + d, 4)) for d in range(1, 4)]
+    m_next = dev_lm(z, ll, lax.rem(ml + 1, 4))
+    m_prev = dev_lm(z, ll, lax.rem(ml + 3, 4))
     right = dev_lm(z, lax.rem(ll + 1, 4), ml)
     left = dev_lm(z, lax.rem(ll + 3, 4), ml)
 
     barrier = pltpu.get_barrier_semaphore()
     with scope("barrier"):
-        peers = [sib, right, left] + m_peers + z_peers
+        peers = [sib, right, left, m_next, m_prev] + z_peers
         for p in peers:
             pl.semaphore_signal(barrier, inc=1, device_id=(p,), device_id_type=MESH)
         pl.semaphore_wait(barrier, len(peers))
@@ -82,16 +83,34 @@
 
     lp, lm, lf = lax.rem(ll + 1, 4), lax.rem(ll + 3, 4), lax.rem(ll + 2, 4)
 
-    for d in range(1, 4):
-        rcopy(xs.at[mine], xs.at[mine], y_send.at[0], y_recv.at[3 - d], m_peers[d - 1]).start()
+    def to_mid(ref, e, p):
+        return rcopy(ref, ref, y_send.at[0], y_recv.at[e], p)
+
+    def half(j, h):
+        return col(ll, j).at[4 * h:4 * h + 4]
+
+    to_mid(xs.at[mine], 1, m_next).start()
+    to_mid(xs.at[mine], 0, m_prev).start()
     to_right(ll, 0, 0).start()
     to_left(ll, 0, 0).start()
 
-    def mid(j, off):
-        with scope("second"):
-            rcopy(col(ll, j), col(ll, j), y_send.at[0], y_recv.at[off - 1], sib).wait_recv()
-        to_right(ll, j, j).start()
-        to_left(ll, j, j).start()
+    with scope("second"):
+        to_mid(col(ll, 1), 0, sib).wait_recv()
+    to_mid(half(1, 0), 2, m_prev).start()
+    to_right(ll, 1, 1).start()
+    to_left(ll, 1, 1).start()
+    with scope("second"):
+        to_mid(col(ll, 2), 1, sib).wait_recv()
+    to_mid(half(2, 1), 3, m_next).start()
+    to_right(ll, 2, 2).start()
+    to_left(ll, 2, 2).start()
+
+    def far_column():
+        with scope("third"):
+            to_mid(half(3, 0), 2, sib).wait_recv()
+            to_mid(half(3, 1), 3, sib).wait_recv()
+        to_right(ll, 3, 3).start()
+        to_left(ll, 3, 3).start()
 
     def event(e):
         to_right(lm, e, e).wait_recv()
@@ -107,13 +126,16 @@
             to_left(lp, e, 2 + e).start()
 
     def unit_of(lc, mc, u):
+        own_u = jnp.logical_or(u == 0, u == 2)
         far = u >= 6
-        odd = lax.rem(u, 2) == 1
-        dl = jnp.where(u < 2, 0, jnp.where(far, 2, jnp.where(odd, 1, 3)))
-        second = jnp.logical_or(jnp.logical_or(u == 1, u == 7), jnp.logical_or(u == 4, u == 5))
-        m1 = lax.rem(mc + jnp.where(second, 3, 0), 4)
-        m2 = lax.rem(mc + jnp.where(second, 2, 1), 4)
-        return lax.rem(lc + dl, 4), m1, m2
+        l1 = lax.rem(lc + jnp.where(own_u, 0, jnp.where(far, 2, 3)), 4)
+        l2 = lax.rem(lc + jnp.where(own_u, 0, jnp.where(far, 2, 1)), 4)
+        pair2 = jnp.logical_or(u == 2, u == 7)
+        ring_off = jnp.where(u == 1, 0, jnp.where(u == 3, 1, jnp.where(u == 4, 3, 2)))
+        pair = jnp.logical_or(own_u, far)
+        m1 = lax.rem(mc + jnp.where(pair, jnp.where(pair2, 3, 0), ring_off), 4)
+        m2 = lax.rem(mc + jnp.where(pair, jnp.where(pair2, 2, 1), ring_off), 4)
+        return (l1, m1), (l2, m2)
 
     load_w.wait()
     load_g.wait()
@@ -122,8 +144,7 @@
     pos = place.astype(F32) / (256 * 512.0)
 
     def project(u):
-        lc, m1, m2 = unit_of(ll, ml, u)
-        rows = jnp.concatenate([xs[column(lc, m1)].reshape(128, 512), xs[column(lc, m2)].reshape(128, 512)], axis=0)
+        rows = jnp.concatenate([xs[column(lc, mc)].reshape(128, 512) for lc, mc in unit_of(ll, ml, u)], axis=0)
         proj = jnp.dot(rows, wv[...], preferred_element_type=F32)
         inv = 1.0 / jnp.sqrt(jnp.sum(proj * proj, axis=1, keepdims=True))
         qown[u] = (proj * inv).astype(BF16)
@@ -147,15 +168,13 @@
         for i, gq in enumerate(groups):
             rows = slice(i * 128, i * 128 + 128)
             e_ref[gq] = ev[rows]
-            stat[gq] = cols[rows].T[:8]
+            stat[gq] = cols[rows].T[:4]
 
     def groups_own(u):
-        lc, m1, m2 = unit_of(ll, ml, u)
-        return [jnp.where(core0, m * 8 + lc * 2, lc * 8 + m * 2 + 1) for m in (m1, m2)]
+        return [jnp.where(core0, mc * 8 + lc * 2, lc * 8 + mc * 2 + 1) for lc, mc in unit_of(ll, ml, u)]
 
     def groups_sib(u):
-        lc, m1, m2 = unit_of(ml, ll, u)
-        return [jnp.where(core0, lc * 8 + m * 2 + 1, m * 8 + lc * 2) for m in (m1, m2)]
+        return [jnp.where(core0, lc * 8 + mc * 2 + 1, mc * 8 + lc * 2) for lc, mc in unit_of(ml, ll, u)]
 
     def groups_both(uo, us):
         return groups_own(uo) + groups_sib(us)
@@ -179,22 +198,20 @@
             send_group(gq)
         return carry
 
-    mid(1, 1)
-    mid(2, 3)
     project(0)
     to_sib(0).start()
-    mid(3, 2)
     with scope("event0"):
         event(0)
     project(1)
     dots(da, [qown[0]])
     to_sib(1).start()
+    far_column()
 
     def step(k, now, before, first):
         with scope("events"):
-            @pl.when(k <= 4)
+            @pl.when(jnp.logical_and(k >= 3, k <= 5))
             def _():
-                event(k - 1)
+                event(k - 2)
 
             @pl.when(k == 6)
             def _():
@@ -261,7 +278,7 @@
         wgt = jnp.exp2((ms - m) * k2)
         return m, jnp.sum(wgt * ref[:, 1, :], axis=0, keepdims=True), jnp.sum(wgt * ref[:, 2, :], axis=0, keepdims=True)
 
-    sub = lax.broadcasted_iota(jnp.int32, (8, 128), 0)
+    sub = lax.broadcasted_iota(jnp.int32, (4, 128), 0)
 
     def tile(a, b, d):
         return jnp.where(sub == 0, a, jnp.where(sub == 1, b, d))
@@ -343,8 +360,8 @@
             scratch_shapes=[
                 VM((16, NZ, 16, 512), BF16), VM((512, 1024), BF16), VM((512, 1024), BF16),
                 VM((8, 256, 1024), BF16), VM((8, 256, 1024), BF16), VM((512, 512), F32), VM((512, 512), F32),
-                VM((32, 8, 128), F32), VM((32, 8, 128), F32), VM((NZ, 8, 128), F32), VM((32, 8, 128), F32),
-                D((3,)), D((2,)), D((1,)), D((3,)), D((1,)), D((6,)), D((1,)), D((6,)),
+                VM((32, 4, 128), F32), VM((32, 4, 128), F32), VM((NZ, 4, 128), F32), VM((32, 4, 128), F32),
+                D((3,)), D((2,)), D((1,)), D((4,)), D((1,)), D((6,)), D((1,)), D((6,)),
                 D((1,)), D((8,)), D((3,)), D((3,)),
             ],
             compiler_params=pltpu.CompilerParams(collective_id=0, has_side_effects=True,

time: 56.9 us -> 56.1 us (0.986)
  Pallas kernels: 55.5 us -> 54.8 us
    pallas_call x1, Pallas kernels: 52.7 us -> 51.9 us  [per_device(): pl.pallas_call(gather_score_kernel, out_shape=(VM((32, 128, 512), F32), V...]
where the time goes in v5:
time: 56.1 us
  Pallas kernels  54.8 us (98%)
  between operations  1.28 us (2%)
    pallas_call x1, Pallas kernels, per_device(): pl.pallas_call(gather_score_kernel, out_shape=(VM((32, 128, 512), F32), V...  51.9 us
    pallas_call x1, Pallas kernels, per_device(): pl.pallas_call(normalise_kernel, out_shape=(jax.ShapeDtypeStruct((NZ, 32,...  2.82 us

profile of v5, /device:TPU:1, one launch (start us, length us, event | category | flops | bytes accessed | tf_op | source)
XLA Modules:
  0.0 56.1 jit_solution(3200702022036719008)
XLA Ops:
  1.3 51.9 %shard_map.59 = (f32[32,128,512]{2,1,0:T(8,128)S(1)}, f32[32,128]{1,0:T(8,128)S(1)}, f32[32,128]{1,0:T(8,128)S(1)}) custom-call(bf16[16,512]{1,0:T(8,128)(2,1)} %x_hbm.1, bf16[512,1024]{1,0:T(8,128)(2,1)} %w_hbm.1, bf16[512,1024]{1,0:T(8,128)(2,1)} %g_hbm.1, f32[1]{0:T(128)S(6)} %copy.6.t_ref), custom_call_target="tpu_custom_call" | custom-call | tf_op jit(solution)/shard_map/pallas_call | solution.py:355
  53.2 2.8 %shard_map.60 = (bf16[8,32,16,512]{3,2,1,0:T(8,128)(2,1)}, f32[32,128]{1,0:T(8,128)}) custom-call(f32[32,128,512]{2,1,0:T(8,128)S(1)} %get-tuple-element.7.e_ref, f32[32,128]{1,0:T(8,128)S(1)} %get-tuple-element.8.fac_ref, f32[32,128]{1,0:T(8,128)S(1)} %get-tuple-element.9.rank_ref), custom_call_target="tpu_custom_call" | custom-call | tf_op jit(solution)/shard_map/pallas_call | solution.py:370

commit v6 on v5

--- a/solution.py
+++ b/solution.py
@@ -18,9 +18,9 @@
                                         device_id=(p,), device_id_type=MESH)
 
 
-def gather_score_kernel(x_hbm, w_hbm, g_hbm, t_ref,
+def gather_score_kernel(x_hbm, w_hbm, g_hbm, t_hbm,
                         e_ref, fac_ref, rank_ref,
-                        xs, wv, gv, qown, qsib, da, db, stat, part, zpart, done,
+                        xs, wv, gv, tv, qown, qsib, da, db, stat, part, zpart, done,
                         in_sem, a_sem, y_send, y_recv, r_send, r_recv, l_send, l_recv,
                         q_send, q_recv, s_send, s_recv):
     me = lax.axis_index("ga")
@@ -47,7 +47,9 @@
     load_x = pltpu.make_async_copy(x_hbm, own, in_sem.at[0])
     load_w = pltpu.make_async_copy(w_hbm, wv, in_sem.at[1])
     load_g = pltpu.make_async_copy(g_hbm, gv, in_sem.at[2])
+    load_t = pltpu.make_async_copy(t_hbm, tv, in_sem.at[3])
     load_x.start()
+    load_t.start()
     load_w.start()
     load_g.start()
 
@@ -71,75 +73,73 @@
     with scope("first"):
         rcopy(xs.at[0, 0:7], xs.at[0, 0:7], a_sem.at[0], a_sem.at[1], sib).wait_recv()
 
-    def col(lc, j):
-        off = jnp.where(j == 0, 0, jnp.where(j == 1, 1, jnp.where(j == 2, 3, 2)))
-        return xs.at[column(lc, lax.rem(ml + off, 4))]
-
-    def to_right(lc, j, e):
-        return rcopy(col(lc, j), col(lc, j), r_send.at[0], r_recv.at[e], right)
-
-    def to_left(lc, j, e):
-        return rcopy(col(lc, j), col(lc, j), l_send.at[0], l_recv.at[e], left)
+    OFF = (0, 1, 3, 2)
+
+    def col(lc, j, h):
+        return xs.at[column(lc, lax.rem(ml + OFF[j], 4)), 4 * h:4 * h + 4]
+
+    def to_right(lc, j, h, far=0):
+        return rcopy(col(lc, j, h), col(lc, j, h), r_send.at[0], r_recv.at[far * 8 + j * 2 + h], right)
+
+    def to_left(lc, j, h, far=0):
+        return rcopy(col(lc, j, h), col(lc, j, h), l_send.at[0], l_recv.at[far * 4 + j * 2 + h], left)
+
+    def to_mid(j, h, e, p):
+        return rcopy(col(ll, j, h), col(ll, j, h), y_send.at[0], y_recv.at[e], p)
 
     lp, lm, lf = lax.rem(ll + 1, 4), lax.rem(ll + 3, 4), lax.rem(ll + 2, 4)
 
-    def to_mid(ref, e, p):
-        return rcopy(ref, ref, y_send.at[0], y_recv.at[e], p)
-
-    def half(j, h):
-        return col(ll, j).at[4 * h:4 * h + 4]
-
-    to_mid(xs.at[mine], 1, m_next).start()
-    to_mid(xs.at[mine], 0, m_prev).start()
-    to_right(ll, 0, 0).start()
-    to_left(ll, 0, 0).start()
+    def round_ring(j, h):
+        to_right(ll, j, h).start()
+        to_left(ll, j, h).start()
+
+    for h in range(2):
+        to_mid(0, h, h, m_prev).start()
+        to_mid(0, 1 - h, 3 - h, m_next).start()
+    round_ring(0, 0)
+    round_ring(0, 1)
 
     with scope("second"):
-        to_mid(col(ll, 1), 0, sib).wait_recv()
-    to_mid(half(1, 0), 2, m_prev).start()
-    to_right(ll, 1, 1).start()
-    to_left(ll, 1, 1).start()
+        to_mid(1, 0, 0, sib).wait_recv()
+    to_mid(1, 0, 4, m_prev).start()
+    round_ring(1, 0)
     with scope("second"):
-        to_mid(col(ll, 2), 1, sib).wait_recv()
-    to_mid(half(2, 1), 3, m_next).start()
-    to_right(ll, 2, 2).start()
-    to_left(ll, 2, 2).start()
+        to_mid(2, 1, 3, sib).wait_recv()
+    to_mid(2, 1, 5, m_next).start()
+    round_ring(2, 1)
+    with scope("second"):
+        to_mid(1, 1, 1, sib).wait_recv()
+    round_ring(1, 1)
+    with scope("second"):
+        to_mid(2, 0, 2, sib).wait_recv()
+    round_ring(2, 0)
 
     def far_column():
-        with scope("third"):
-            to_mid(half(3, 0), 2, sib).wait_recv()
-            to_mid(half(3, 1), 3, sib).wait_recv()
-        to_right(ll, 3, 3).start()
-        to_left(ll, 3, 3).start()
-
-    def event(e):
-        to_right(lm, e, e).wait_recv()
-
-        @pl.when(e < 2)
-        def _():
-            to_right(lm, e, 4 + e).start()
-
-        to_left(lp, e, e).wait_recv()
-
-        @pl.when(e >= 2)
-        def _():
-            to_left(lp, e, 2 + e).start()
+        for h in range(2):
+            with scope("third"):
+                to_mid(3, h, 4 + h, sib).wait_recv()
+            round_ring(3, h)
+
+    def event(j):
+        for i in range(2):
+            h = 1 - i if j == 2 else i
+            to_right(lm, j, h).wait_recv()
+            if j < 2:
+                to_right(lm, j, h, 1).start()
+            to_left(lp, j, h).wait_recv()
+            if j >= 2:
+                to_left(lp, j, h, 1).start()
+
+    UNITS = (((0, 0), (0, 1)), ((3, 0), (1, 0)), ((0, 3), (0, 2)), ((3, 1), (1, 1)),
+             ((3, 3), (1, 3)), ((3, 2), (1, 2)), ((2, 0), (2, 1)), ((2, 3), (2, 2)))
 
     def unit_of(lc, mc, u):
-        own_u = jnp.logical_or(u == 0, u == 2)
-        far = u >= 6
-        l1 = lax.rem(lc + jnp.where(own_u, 0, jnp.where(far, 2, 3)), 4)
-        l2 = lax.rem(lc + jnp.where(own_u, 0, jnp.where(far, 2, 1)), 4)
-        pair2 = jnp.logical_or(u == 2, u == 7)
-        ring_off = jnp.where(u == 1, 0, jnp.where(u == 3, 1, jnp.where(u == 4, 3, 2)))
-        pair = jnp.logical_or(own_u, far)
-        m1 = lax.rem(mc + jnp.where(pair, jnp.where(pair2, 3, 0), ring_off), 4)
-        m2 = lax.rem(mc + jnp.where(pair, jnp.where(pair2, 2, 1), ring_off), 4)
-        return (l1, m1), (l2, m2)
+        return [(lax.rem(lc + a, 4), lax.rem(mc + b, 4)) for a, b in UNITS[u]]
 
     load_w.wait()
     load_g.wait()
-    k2 = jnp.minimum(jnp.exp(jnp.full((1, 1), t_ref[0], F32)) * LOG2E, F32_MAX)
+    load_t.wait()
+    k2 = jnp.minimum(jnp.exp(jnp.full((1, 1), tv[0], F32)) * LOG2E, F32_MAX)
     place = lax.broadcasted_iota(jnp.int32, (1, 512), 1) + me * 512
     pos = place.astype(F32) / (256 * 512.0)
 
@@ -188,15 +188,13 @@
         def _():
             part[pi] = stat[pi]
 
-    def send_own(u, carry):
+    def send_own(u):
         for gq in groups_own(u):
             send_group(gq)
-        return carry
-
-    def send_sib(u, carry):
+
+    def send_sib(u):
         for gq in groups_sib(u):
             send_group(gq)
-        return carry
 
     project(0)
     to_sib(0).start()
@@ -207,67 +205,50 @@
     to_sib(1).start()
     far_column()
 
-    def step(k, now, before, first):
+    def step(k, now, before):
         with scope("events"):
-            @pl.when(jnp.logical_and(k >= 3, k <= 5))
-            def _():
+            if 3 <= k <= 5:
                 event(k - 2)
-
-            @pl.when(k == 6)
-            def _():
-                for e in range(4, 6):
-                    to_right(lf, e - 4, e).wait_recv()
-
-            @pl.when(k == 7)
-            def _():
-                for e in range(4, 6):
-                    to_left(lf, e - 2, e).wait_recv()
+            for h in range(2):
+                if k == 6:
+                    to_right(lf, 0, h, 1).wait_recv()
+                    to_right(lf, 1, h, 1).wait_recv()
+                if k == 7:
+                    to_left(lf, 2, h, 1).wait_recv()
+                    to_left(lf, 3, h, 1).wait_recv()
 
         with scope("sibwait"):
             to_sib(k - 2).wait_recv()
         with scope("compute"):
-            soften(before, groups_own(0) if first else groups_both(k - 2, k - 3))
+            soften(before, groups_own(0) if k == 2 else groups_both(k - 2, k - 3))
             project(k)
             dots(now, [qown[k - 1], qsib[k - 2]])
         to_sib(k).start()
 
-    step(2, db, da, True)
-    step(3, da, db, False)
-
-    def body(i, carry):
-        k = 2 * i
-        step(k, db, da, False)
-
-        @pl.when(i == 3)
-        def _():
-            lax.fori_loop(0, 4, send_own, 0)
-            lax.fori_loop(0, 3, send_sib, 0)
-
-        step(k + 1, da, db, False)
-
-        @pl.when(i == 3)
-        def _():
-            lax.fori_loop(4, 6, send_own, 0)
-            lax.fori_loop(3, 5, send_sib, 0)
-
-        return carry
-
-    lax.fori_loop(2, 4, body, 0)
+    for k in range(2, 8):
+        step(k, db if k % 2 == 0 else da, da if k % 2 == 0 else db)
+        if k >= 6:
+            for u in range(0 if k == 6 else 4, k - 2):
+                send_own(u)
+            for u in range(0 if k == 6 else 3, k - 3):
+                send_sib(u)
+    send_own(5)
+    send_sib(4)
     with scope("tail6"):
         to_sib(6).wait_recv()
         soften(da, groups_both(6, 5))
         dots(db, [qown[7], qsib[6]])
-    send_own(6, 0)
-    send_sib(5, 0)
+    send_own(6)
+    send_sib(5)
     with scope("tail7"):
         to_sib(7).wait_recv()
         soften(db, groups_both(7, 6))
         dots(da, [qsib[7]])
-    send_own(7, 0)
-    send_sib(6, 0)
+    send_own(7)
+    send_sib(6)
     with scope("tail8"):
         soften(da, groups_sib(7))
-    send_sib(7, 0)
+    send_sib(7)
 
     with scope("s1wait"):
         rcopy(part.at[0:31], part.at[0:31], s_send.at[0], s_recv.at[0], sib).wait_recv()
@@ -291,13 +272,12 @@
     m, zs, rs = merge(zpart)
     done[pi] = tile(m, 1.0 / zs, rs / zs)
 
-    def send_done(k, carry):
-        p = lax.rem(pi + k, 32)
-        rcopy(done.at[pi], done.at[pi], s_send.at[2], s_recv.at[2], z * 32 + p).start()
-        return carry
-
+    peers = [(dy, dx, dc) for dy in range(4) for dx in range(4) for dc in range(2)][1:]
+    peers.sort(key=lambda p: -min(p[0], 4 - p[0]) - min(p[1], 4 - p[1]))
     with scope("s3send"):
-        lax.fori_loop(1, 32, send_done, 0)
+        for dy, dx, dc in peers:
+            p = dev(z, lax.rem(y + dy, NY), lax.rem(x + dx, NX), lax.rem(c + dc, NC))
+            rcopy(done.at[pi], done.at[pi], s_send.at[2], s_recv.at[2], p).start()
 
     with scope("s3wait"):
         rcopy(done.at[0:31], done.at[0:31], s_send.at[2], s_recv.at[2], sib).wait_recv()
@@ -355,13 +335,13 @@
         e, fac, rank = pl.pallas_call(
             gather_score_kernel,
             out_shape=(VM((32, 128, 512), F32), VM((32, 128), F32), VM((32, 128), F32)),
-            in_specs=[pl.BlockSpec(memory_space=pl.ANY)] * 3 + [pl.BlockSpec(memory_space=pltpu.SMEM)],
+            in_specs=[pl.BlockSpec(memory_space=pl.ANY)] * 4,
             out_specs=(pl.BlockSpec(memory_space=VM),) * 3,
             scratch_shapes=[
                 VM((16, NZ, 16, 512), BF16), VM((512, 1024), BF16), VM((512, 1024), BF16),
-                VM((8, 256, 1024), BF16), VM((8, 256, 1024), BF16), VM((512, 512), F32), VM((512, 512), F32),
+                pltpu.SMEM((1,), F32), VM((8, 256, 1024), BF16), VM((8, 256, 1024), BF16), VM((512, 512), F32), VM((512, 512), F32),
                 VM((32, 4, 128), F32), VM((32, 4, 128), F32), VM((NZ, 4, 128), F32), VM((32, 4, 128), F32),
-                D((3,)), D((2,)), D((1,)), D((4,)), D((1,)), D((6,)), D((1,)), D((6,)),
+                D((4,)), D((2,)), D((1,)), D((6,)), D((1,)), D((12,)), D((1,)), D((12,)),
                 D((1,)), D((8,)), D((3,)), D((3,)),
             ],
             compiler_params=pltpu.CompilerParams(collective_id=0, has_side_effects=True,

time: 56.1 us -> 54.3 us (0.968)
  Pallas kernels: 54.8 us -> 52.9 us
    pallas_call x1, Pallas kernels: 51.9 us -> 50.1 us  [per_device(): pl.pallas_call(gather_score_kernel, out_shape=(VM((32, 128, 512), F32), V...]
where the time goes in v6:
time: 54.3 us; the launch traced here: 54.2 us
  Pallas kernels  52.9 us (97%)
  between operations  1.28 us (2%)
    pallas_call x1, Pallas kernels, per_device(): pl.pallas_call(gather_score_kernel, out_shape=(VM((32, 128, 512), F32), V...  50.1 us
    pallas_call x1, Pallas kernels, per_device(): pl.pallas_call(normalise_kernel, out_shape=(jax.ShapeDtypeStruct((NZ, 32,...  2.82 us

profile of v6, /device:TPU:1, one launch (start us, length us, event | category | flops | bytes accessed | tf_op | source)
XLA Modules:
  0.0 54.2 jit_solution(15098082486618945131)
XLA Ops:
  1.3 50.1 %shard_map.59 = (f32[32,128,512]{2,1,0:T(8,128)S(1)}, f32[32,128]{1,0:T(8,128)S(1)}, f32[32,128]{1,0:T(8,128)S(1)}) custom-call(bf16[16,512]{1,0:T(8,128)(2,1)} %x_hbm.1, bf16[512,1024]{1,0:T(8,128)(2,1)} %w_hbm.1, bf16[512,1024]{1,0:T(8,128)(2,1)} %g_hbm.1, f32[1]{0:T(128)S(6)} %copy.6.t_hbm), custom_call_target="tpu_custom_call" | custom-call | tf_op jit(solution)/shard_map/pallas_call | solution.py:335
  51.4 2.8 %shard_map.60 = (bf16[8,32,16,512]{3,2,1,0:T(8,128)(2,1)}, f32[32,128]{1,0:T(8,128)}) custom-call(f32[32,128,512]{2,1,0:T(8,128)S(1)} %get-tuple-element.7.e_ref, f32[32,128]{1,0:T(8,128)S(1)} %get-tuple-element.8.fac_ref, f32[32,128]{1,0:T(8,128)S(1)} %get-tuple-element.9.rank_ref), custom_call_target="tpu_custom_call" | custom-call | tf_op jit(solution)/shard_map/pallas_call | solution.py:350

commit v7 on v6

--- a/solution.py
+++ b/solution.py
@@ -68,7 +68,8 @@
         pl.semaphore_wait(barrier, len(peers))
         load_x.wait()
 
-    for d in range(1, NZ):
+    FAR_FIRST = (4, 3, 5, 2, 6, 1, 7)
+    for d in FAR_FIRST:
         rcopy(own, own, a_sem.at[0], a_sem.at[1], z_peers[d - 1]).start()
     with scope("first"):
         rcopy(xs.at[0, 0:7], xs.at[0, 0:7], a_sem.at[0], a_sem.at[1], sib).wait_recv()
@@ -179,14 +180,19 @@
     def groups_both(uo, us):
         return groups_own(uo) + groups_sib(us)
 
+    def antipode(p):
+        return lax.rem(p // 8 + 2, 4) * 8 + lax.rem(lax.rem(p, 8) + 4, 8)
+
+    gm = antipode(pi)
+
     def send_group(gq):
-        @pl.when(gq != pi)
+        @pl.when(gq != gm)
         def _():
-            rcopy(stat.at[gq], part.at[pi], s_send.at[0], s_recv.at[0], z * 32 + gq).start()
-
-        @pl.when(gq == pi)
+            rcopy(stat.at[gq], part.at[pi], s_send.at[0], s_recv.at[0], z * 32 + antipode(gq)).start()
+
+        @pl.when(gq == gm)
         def _():
-            part[pi] = stat[pi]
+            part[pi] = stat[gm]
 
     def send_own(u):
         for gq in groups_own(u):
@@ -219,18 +225,24 @@
 
         with scope("sibwait"):
             to_sib(k - 2).wait_recv()
+        if k == 7:
+            with scope("project"):
+                project(k)
+            to_sib(k).start()
         with scope("compute"):
             soften(before, groups_own(0) if k == 2 else groups_both(k - 2, k - 3))
-            project(k)
+            if k < 7:
+                project(k)
             dots(now, [qown[k - 1], qsib[k - 2]])
-        to_sib(k).start()
+        if k < 7:
+            to_sib(k).start()
 
     for k in range(2, 8):
         step(k, db if k % 2 == 0 else da, da if k % 2 == 0 else db)
         if k >= 6:
             for u in range(0 if k == 6 else 4, k - 2):
                 send_own(u)
-            for u in range(0 if k == 6 else 3, k - 3):
+            for u in (2,) if k == 6 else (0, 1, 3):
                 send_sib(u)
     send_own(5)
     send_sib(4)
@@ -265,19 +277,19 @@
         return jnp.where(sub == 0, a, jnp.where(sub == 1, b, d))
 
     zpart[z] = tile(*merge(part))
-    for d in range(1, NZ):
+    for d in FAR_FIRST:
         rcopy(zpart.at[z], zpart.at[z], s_send.at[1], s_recv.at[1], z_peers[d - 1]).start()
     with scope("s2wait"):
         rcopy(zpart.at[0:7], zpart.at[0:7], s_send.at[1], s_recv.at[1], sib).wait_recv()
     m, zs, rs = merge(zpart)
-    done[pi] = tile(m, 1.0 / zs, rs / zs)
+    done[gm] = tile(m, 1.0 / zs, rs / zs)
 
     peers = [(dy, dx, dc) for dy in range(4) for dx in range(4) for dc in range(2)][1:]
     peers.sort(key=lambda p: -min(p[0], 4 - p[0]) - min(p[1], 4 - p[1]))
     with scope("s3send"):
         for dy, dx, dc in peers:
             p = dev(z, lax.rem(y + dy, NY), lax.rem(x + dx, NX), lax.rem(c + dc, NC))
-            rcopy(done.at[pi], done.at[pi], s_send.at[2], s_recv.at[2], p).start()
+            rcopy(done.at[gm], done.at[gm], s_send.at[2], s_recv.at[2], p).start()
 
     with scope("s3wait"):
         rcopy(done.at[0:31], done.at[0:31], s_send.at[2], s_recv.at[2], sib).wait_recv()

time: 54.3 us -> 52.2 us (0.961)
  Pallas kernels: 52.9 us -> 50.8 us
    pallas_call x1, Pallas kernels: 50.1 us -> 48 us  [per_device(): pl.pallas_call(gather_score_kernel, out_shape=(VM((32, 128, 512), F32), V...]
where the time goes in v7:
time: 52.2 us; the launch traced here: 52.1 us
  Pallas kernels  50.8 us (97%)
  between operations  1.28 us (2%)
    pallas_call x1, Pallas kernels, per_device(): pl.pallas_call(gather_score_kernel, out_shape=(VM((32, 128, 512), F32), V...  48 us
    pallas_call x1, Pallas kernels, per_device(): pl.pallas_call(normalise_kernel, out_shape=(jax.ShapeDtypeStruct((NZ, 32,...  2.82 us

profile of v7, /device:TPU:1, one launch (start us, length us, event | category | flops | bytes accessed | tf_op | source)
XLA Modules:
  0.0 52.1 jit_solution(4783529795856623355)
XLA Ops:
  1.3 48.0 %shard_map.59 = (f32[32,128,512]{2,1,0:T(8,128)S(1)}, f32[32,128]{1,0:T(8,128)S(1)}, f32[32,128]{1,0:T(8,128)S(1)}) custom-call(bf16[16,512]{1,0:T(8,128)(2,1)} %x_hbm.1, bf16[512,1024]{1,0:T(8,128)(2,1)} %w_hbm.1, bf16[512,1024]{1,0:T(8,128)(2,1)} %g_hbm.1, f32[1]{0:T(128)S(6)} %copy.6.t_hbm), custom_call_target="tpu_custom_call" | custom-call | tf_op jit(solution)/shard_map/pallas_call | solution.py:347
  49.2 2.8 %shard_map.60 = (bf16[8,32,16,512]{3,2,1,0:T(8,128)(2,1)}, f32[32,128]{1,0:T(8,128)}) custom-call(f32[32,128,512]{2,1,0:T(8,128)S(1)} %get-tuple-element.7.e_ref, f32[32,128]{1,0:T(8,128)S(1)} %get-tuple-element.8.fac_ref, f32[32,128]{1,0:T(8,128)S(1)} %get-tuple-element.9.rank_ref), custom_call_target="tpu_custom_call" | custom-call | tf_op jit(solution)/shard_map/pallas_call | solution.py:362

commit v8 on v7

--- a/solution.py
+++ b/solution.py
@@ -69,15 +69,15 @@
         load_x.wait()
 
     FAR_FIRST = (4, 3, 5, 2, 6, 1, 7)
+    near = z // 4
     for d in FAR_FIRST:
-        rcopy(own, own, a_sem.at[0], a_sem.at[1], z_peers[d - 1]).start()
-    with scope("first"):
-        rcopy(xs.at[0, 0:7], xs.at[0, 0:7], a_sem.at[0], a_sem.at[1], sib).wait_recv()
+        same = lax.rem(z + d, NZ) // 4 == near
+        rcopy(own, own, a_sem.at[0], a_sem.at[jnp.where(same, 1, 2)], z_peers[d - 1]).start()
 
     OFF = (0, 1, 3, 2)
 
     def col(lc, j, h):
-        return xs.at[column(lc, lax.rem(ml + OFF[j], 4)), 4 * h:4 * h + 4]
+        return xs.at[column(lc, lax.rem(ml + OFF[j], 4)), pl.ds(4 * (near if h == 0 else 1 - near), 4)]
 
     def to_right(lc, j, h, far=0):
         return rcopy(col(lc, j, h), col(lc, j, h), r_send.at[0], r_recv.at[far * 8 + j * 2 + h], right)
@@ -95,25 +95,27 @@
         to_left(ll, j, h).start()
 
     for h in range(2):
+        with scope("first"):
+            got = xs.at[0, 0:3 + h]
+            rcopy(got, got, a_sem.at[0], a_sem.at[1 + h], sib).wait_recv()
         to_mid(0, h, h, m_prev).start()
-        to_mid(0, 1 - h, 3 - h, m_next).start()
-    round_ring(0, 0)
-    round_ring(0, 1)
+        to_mid(0, h, 2 + h, m_next).start()
+        round_ring(0, h)
 
     with scope("second"):
         to_mid(1, 0, 0, sib).wait_recv()
     to_mid(1, 0, 4, m_prev).start()
     round_ring(1, 0)
     with scope("second"):
+        to_mid(2, 0, 2, sib).wait_recv()
+    round_ring(2, 0)
+    with scope("second"):
         to_mid(2, 1, 3, sib).wait_recv()
     to_mid(2, 1, 5, m_next).start()
-    round_ring(2, 1)
     with scope("second"):
         to_mid(1, 1, 1, sib).wait_recv()
     round_ring(1, 1)
-    with scope("second"):
-        to_mid(2, 0, 2, sib).wait_recv()
-    round_ring(2, 0)
+    round_ring(2, 1)
 
     def far_column():
         for h in range(2):
@@ -122,8 +124,7 @@
             round_ring(3, h)
 
     def event(j):
-        for i in range(2):
-            h = 1 - i if j == 2 else i
+        for h in range(2):
             to_right(lm, j, h).wait_recv()
             if j < 2:
                 to_right(lm, j, h, 1).start()
@@ -311,16 +312,17 @@
 
 
 def normalise_kernel(e_ref, fac_ref, rank_ref, p_hbm, r_ref, buf, sem):
+    def out(i):
+        return pltpu.make_async_copy(buf.at[:, pl.ds(8 * i, 8)], p_hbm.at[:, pl.ds(8 * i, 8)], sem.at[i])
+
     def body(i, carry):
         for j in range(8):
             gq = i * 8 + j
             f = jnp.broadcast_to(fac_ref[pl.ds(gq, 1), :], (128, 128)).T
             ev = e_ref[gq]
             p = jnp.concatenate([ev[:, b * 128:(b + 1) * 128] * f for b in range(4)], axis=1)
-            buf[gq] = p.astype(BF16).reshape(8, 16, 512)
-        for j in range(8):
-            gq = i * 8 + j
-            pltpu.make_async_copy(buf.at[gq], p_hbm.at[:, gq], sem.at[i]).start()
+            buf[:, gq] = p.astype(BF16).reshape(8, 16, 512)
+        out(i).start()
         return carry
 
     lax.fori_loop(0, 4, body, 0)
@@ -336,7 +338,7 @@
         r_ref[pl.ds(yy, 8, stride=4), :] = nat
 
     for i in range(4):
-        pltpu.make_async_copy(buf.at[0:8], p_hbm.at[:, 0:8], sem.at[i]).wait()
+        out(i).wait()
 
 
 def solution(mesh):
@@ -353,7 +355,7 @@
                 VM((16, NZ, 16, 512), BF16), VM((512, 1024), BF16), VM((512, 1024), BF16),
                 pltpu.SMEM((1,), F32), VM((8, 256, 1024), BF16), VM((8, 256, 1024), BF16), VM((512, 512), F32), VM((512, 512), F32),
                 VM((32, 4, 128), F32), VM((32, 4, 128), F32), VM((NZ, 4, 128), F32), VM((32, 4, 128), F32),
-                D((4,)), D((2,)), D((1,)), D((6,)), D((1,)), D((12,)), D((1,)), D((12,)),
+                D((4,)), D((3,)), D((1,)), D((6,)), D((1,)), D((12,)), D((1,)), D((12,)),
                 D((1,)), D((8,)), D((3,)), D((3,)),
             ],
             compiler_params=pltpu.CompilerParams(collective_id=0, has_side_effects=True,
@@ -364,7 +366,7 @@
             out_shape=(jax.ShapeDtypeStruct((NZ, 32, 16, 512), BF16), jax.ShapeDtypeStruct((32, 128), F32)),
             in_specs=[pl.BlockSpec(memory_space=VM)] * 3,
             out_specs=(pl.BlockSpec(memory_space=pl.ANY), pl.BlockSpec(memory_space=VM)),
-            scratch_shapes=[VM((32, NZ, 16, 512), BF16), D((4,))],
+            scratch_shapes=[VM((NZ, 32, 16, 512), BF16), D((4,))],
             compiler_params=pltpu.CompilerParams(vmem_limit_bytes=24 * 1024 * 1024),
         )(e, fac, rank)
         return prob.reshape(4096, 512), rank.reshape(4096)

time: 52.2 us -> 51.7 us (level)
  no operation moved by 1% of the time
where the time goes in v8:
time: 51.7 us
  Pallas kernels  50.4 us (97%)
  between operations  1.28 us (2%)
    pallas_call x1, Pallas kernels, per_device(): pl.pallas_call(gather_score_kernel, out_shape=(VM((32, 128, 512), F32), V...  47.5 us
    pallas_call x1, Pallas kernels, per_device(): pl.pallas_call(normalise_kernel, out_shape=(jax.ShapeDtypeStruct((NZ, 32,...  2.85 us

profile of v8, /device:TPU:1, one launch (start us, length us, event | category | flops | bytes accessed | tf_op | source)
XLA Modules:
  0.0 51.7 jit_solution(14862028957201768289)
XLA Ops:
  1.3 47.5 %shard_map.59 = (f32[32,128,512]{2,1,0:T(8,128)S(1)}, f32[32,128]{1,0:T(8,128)S(1)}, f32[32,128]{1,0:T(8,128)S(1)}) custom-call(bf16[16,512]{1,0:T(8,128)(2,1)} %x_hbm.1, bf16[512,1024]{1,0:T(8,128)(2,1)} %w_hbm.1, bf16[512,1024]{1,0:T(8,128)(2,1)} %g_hbm.1, f32[1]{0:T(128)S(6)} %copy.6.t_hbm), custom_call_target="tpu_custom_call" | custom-call | tf_op jit(solution)/shard_map/pallas_call | solution.py:349
  48.8 2.9 %shard_map.60 = (bf16[8,32,16,512]{3,2,1,0:T(8,128)(2,1)}, f32[32,128]{1,0:T(8,128)}) custom-call(f32[32,128,512]{2,1,0:T(8,128)S(1)} %get-tuple-element.7.e_ref, f32[32,128]{1,0:T(8,128)S(1)} %get-tuple-element.8.fac_ref, f32[32,128]{1,0:T(8,128)S(1)} %get-tuple-element.9.rank_ref), custom_call_target="tpu_custom_call" | custom-call | tf_op jit(solution)/shard_map/pallas_call | solution.py:364

commit v9 on v8

--- a/solution.py
+++ b/solution.py
@@ -102,20 +102,21 @@
         to_mid(0, h, 2 + h, m_next).start()
         round_ring(0, h)
 
-    with scope("second"):
-        to_mid(1, 0, 0, sib).wait_recv()
-    to_mid(1, 0, 4, m_prev).start()
-    round_ring(1, 0)
-    with scope("second"):
-        to_mid(2, 0, 2, sib).wait_recv()
-    round_ring(2, 0)
-    with scope("second"):
-        to_mid(2, 1, 3, sib).wait_recv()
-    to_mid(2, 1, 5, m_next).start()
-    with scope("second"):
-        to_mid(1, 1, 1, sib).wait_recv()
-    round_ring(1, 1)
-    round_ring(2, 1)
+    def mid_columns():
+        with scope("second"):
+            to_mid(1, 0, 0, sib).wait_recv()
+        to_mid(1, 0, 4, m_prev).start()
+        round_ring(1, 0)
+        with scope("second"):
+            to_mid(2, 0, 2, sib).wait_recv()
+        round_ring(2, 0)
+        with scope("second"):
+            to_mid(2, 1, 3, sib).wait_recv()
+        to_mid(2, 1, 5, m_next).start()
+        with scope("second"):
+            to_mid(1, 1, 1, sib).wait_recv()
+        round_ring(1, 1)
+        round_ring(2, 1)
 
     def far_column():
         for h in range(2):
@@ -123,20 +124,53 @@
                 to_mid(3, h, 4 + h, sib).wait_recv()
             round_ring(3, h)
 
-    def event(j):
+    def from_left(j):
         for h in range(2):
             to_right(lm, j, h).wait_recv()
             if j < 2:
                 to_right(lm, j, h, 1).start()
+
+    def from_right(j):
+        for h in range(2):
             to_left(lp, j, h).wait_recv()
             if j >= 2:
                 to_left(lp, j, h, 1).start()
 
-    UNITS = (((0, 0), (0, 1)), ((3, 0), (1, 0)), ((0, 3), (0, 2)), ((3, 1), (1, 1)),
-             ((3, 3), (1, 3)), ((3, 2), (1, 2)), ((2, 0), (2, 1)), ((2, 3), (2, 2)))
+    def far_left(j):
+        for h in range(2):
+            to_right(lf, j, h, 1).wait_recv()
+
+    def far_right(j):
+        for h in range(2):
+            to_left(lf, j, h, 1).wait_recv()
+
+    UNITS = (((0, 0),), ((0, 1), (0, 3)), ((3, 0), (1, 0)), ((0, 2), (3, 1)), ((1, 1), (3, 3)),
+             ((1, 3), (3, 2)), ((1, 2), (2, 0)), ((2, 1), (2, 3)), ((2, 2),))
 
     def unit_of(lc, mc, u):
         return [(lax.rem(lc + a, 4), lax.rem(mc + b, 4)) for a, b in UNITS[u]]
+
+    def events(k):
+        if k == 2:
+            from_left(0)
+            from_right(0)
+        if k == 3:
+            far_column()
+            from_left(1)
+        if k == 4:
+            from_right(1)
+            from_left(2)
+        if k == 5:
+            from_right(2)
+            from_left(3)
+        if k == 6:
+            from_right(3)
+            far_left(0)
+        if k == 7:
+            far_left(1)
+            far_right(2)
+        if k == 8:
+            far_right(3)
 
     load_w.wait()
     load_g.wait()
@@ -145,18 +179,21 @@
     place = lax.broadcasted_iota(jnp.int32, (1, 512), 1) + me * 512
     pos = place.astype(F32) / (256 * 512.0)
 
+    def q_of(ref, u):
+        return ref.at[u, 0:128 * len(UNITS[u])]
+
     def project(u):
         rows = jnp.concatenate([xs[column(lc, mc)].reshape(128, 512) for lc, mc in unit_of(ll, ml, u)], axis=0)
         proj = jnp.dot(rows, wv[...], preferred_element_type=F32)
         inv = 1.0 / jnp.sqrt(jnp.sum(proj * proj, axis=1, keepdims=True))
-        qown[u] = (proj * inv).astype(BF16)
+        q_of(qown, u)[...] = (proj * inv).astype(BF16)
 
     def to_sib(u):
-        return rcopy(qown.at[u], qsib.at[u], q_send.at[0], q_recv.at[u], sib)
-
-    def dots(buf, qs):
-        q = qs[0] if len(qs) == 1 else jnp.concatenate(qs, axis=0)
-        buf[0:256 * len(qs)] = lax.dot_general(q, gv[...], (((1,), (1,)), ((), ())), preferred_element_type=F32)
+        return rcopy(q_of(qown, u), q_of(qsib, u), q_send.at[0], q_recv.at[u], sib)
+
+    def dots(buf, uo, us):
+        q = jnp.concatenate([q_of(qown, u)[...] for u in uo] + [q_of(qsib, u)[...] for u in us], axis=0)
+        buf[0:q.shape[0]] = lax.dot_general(q, gv[...], (((1,), (1,)), ((), ())), preferred_element_type=F32)
 
     def soften(buf, groups):
         n = 128 * len(groups)
@@ -178,8 +215,8 @@
     def groups_sib(u):
         return [jnp.where(core0, lc * 8 + mc * 2 + 1, mc * 8 + lc * 2) for lc, mc in unit_of(ml, ll, u)]
 
-    def groups_both(uo, us):
-        return groups_own(uo) + groups_sib(us)
+    def groups_of(uo, us):
+        return sum([groups_own(u) for u in uo] + [groups_sib(u) for u in us], [])
 
     def antipode(p):
         return lax.rem(p // 8 + 2, 4) * 8 + lax.rem(lax.rem(p, 8) + 4, 8)
@@ -195,73 +232,63 @@
         def _():
             part[pi] = stat[gm]
 
-    def send_own(u):
-        for gq in groups_own(u):
-            send_group(gq)
-
-    def send_sib(u):
-        for gq in groups_sib(u):
-            send_group(gq)
-
-    project(0)
-    to_sib(0).start()
-    with scope("event0"):
-        event(0)
-    project(1)
-    dots(da, [qown[0]])
-    to_sib(1).start()
-    far_column()
-
-    def step(k, now, before):
+    LAST = 8
+
+    def scored(k):
+        return [u for u in (k - 1,) if 0 <= u <= LAST], [u for u in (k - 2,) if 0 <= u <= LAST]
+
+    def step(k):
+        now, before = (da, db) if k % 2 else (db, da)
         with scope("events"):
-            if 3 <= k <= 5:
-                event(k - 2)
-            for h in range(2):
-                if k == 6:
-                    to_right(lf, 0, h, 1).wait_recv()
-                    to_right(lf, 1, h, 1).wait_recv()
-                if k == 7:
-                    to_left(lf, 2, h, 1).wait_recv()
-                    to_left(lf, 3, h, 1).wait_recv()
-
+            events(k)
+        uo, us = scored(k)
         with scope("sibwait"):
-            to_sib(k - 2).wait_recv()
-        if k == 7:
+            for u in us:
+                to_sib(u).wait_recv()
+        if k == LAST:
             with scope("project"):
                 project(k)
             to_sib(k).start()
         with scope("compute"):
-            soften(before, groups_own(0) if k == 2 else groups_both(k - 2, k - 3))
-            if k < 7:
+            if k >= 2:
+                soften(before, groups_of(*scored(k - 1)))
+            if k < LAST:
                 project(k)
-            dots(now, [qown[k - 1], qsib[k - 2]])
-        if k < 7:
+            if uo or us:
+                dots(now, uo, us)
+        if k < LAST:
             to_sib(k).start()
 
-    for k in range(2, 8):
-        step(k, db if k % 2 == 0 else da, da if k % 2 == 0 else db)
-        if k >= 6:
-            for u in range(0 if k == 6 else 4, k - 2):
-                send_own(u)
-            for u in (2,) if k == 6 else (0, 1, 3):
-                send_sib(u)
-    send_own(5)
-    send_sib(4)
+    SENDS = {6: ((0, 1, 2, 3), (1,)), 7: ((4,), (2, 3)), 8: ((5, 6), (0, 4, 5)), 9: ((7,), (6,)), 10: ((8,), (7,)),
+             11: ((), (8,))}
+
+    def sends(k):
+        for u in SENDS[k][0]:
+            for gq in groups_own(u):
+                send_group(gq)
+        for u in SENDS[k][1]:
+            for gq in groups_sib(u):
+                send_group(gq)
+
+    step(0)
+    mid_columns()
+    for k in range(1, LAST + 1):
+        step(k)
+        if k in SENDS:
+            sends(k)
     with scope("tail6"):
-        to_sib(6).wait_recv()
-        soften(da, groups_both(6, 5))
-        dots(db, [qown[7], qsib[6]])
-    send_own(6)
-    send_sib(5)
+        to_sib(LAST - 1).wait_recv()
+        soften(db, groups_of(*scored(LAST)))
+        dots(da, *scored(LAST + 1))
+    sends(LAST + 1)
     with scope("tail7"):
-        to_sib(7).wait_recv()
-        soften(db, groups_both(7, 6))
-        dots(da, [qsib[7]])
-    send_own(7)
-    send_sib(6)
+        to_sib(LAST).wait_recv()
+        soften(da, groups_of(*scored(LAST + 1)))
+        dots(db, *scored(LAST + 2))
+    sends(LAST + 2)
     with scope("tail8"):
-        soften(da, groups_sib(7))
-    send_sib(7)
+        soften(db, groups_of(*scored(LAST + 2)))
+    sends(LAST + 3)
 
     with scope("s1wait"):
         rcopy(part.at[0:31], part.at[0:31], s_send.at[0], s_recv.at[0], sib).wait_recv()
@@ -305,19 +332,19 @@
         sent(xs.at[0:3], y_send.at[0])
         sent(xs.at[0:6], r_send.at[0])
         sent(xs.at[0:6], l_send.at[0])
-        sent(qown, q_send.at[0])
+        sent(qown.at[0:8], q_send.at[0])
         sent(part.at[0:31], s_send.at[0])
         sent(zpart.at[0:7], s_send.at[1])
         sent(done.at[0:31], s_send.at[2])
 
 
-def normalise_kernel(e_ref, fac_ref, rank_ref, p_hbm, r_ref, buf, sem):
+def normalise_kernel(e_ref, fac_ref, rank_ref, p_hbm, r_hbm, buf, nat_ref, sem):
     def out(i):
-        return pltpu.make_async_copy(buf.at[:, pl.ds(8 * i, 8)], p_hbm.at[:, pl.ds(8 * i, 8)], sem.at[i])
+        return pltpu.make_async_copy(buf.at[:, pl.ds(4 * i, 4)], p_hbm.at[:, pl.ds(4 * i, 4)], sem.at[i])
 
     def body(i, carry):
-        for j in range(8):
-            gq = i * 8 + j
+        for j in range(4):
+            gq = i * 4 + j
             f = jnp.broadcast_to(fac_ref[pl.ds(gq, 1), :], (128, 128)).T
             ev = e_ref[gq]
             p = jnp.concatenate([ev[:, b * 128:(b + 1) * 128] * f for b in range(4)], axis=1)
@@ -325,7 +352,7 @@
         out(i).start()
         return carry
 
-    lax.fori_loop(0, 4, body, 0)
+    lax.fori_loop(0, 8, body, 0)
 
     lane = lax.broadcasted_iota(jnp.int32, (8, 128), 1) // 16
     sub = lax.broadcasted_iota(jnp.int32, (8, 128), 0)
@@ -335,10 +362,13 @@
         for d in range(1, 8):
             moved = pltpu.roll(pltpu.roll(r, 16 * d, 1), 8 - d, 0)
             nat = jnp.where(lax.rem(lane - sub + 8, 8) == d, moved, nat)
-        r_ref[pl.ds(yy, 8, stride=4), :] = nat
-
-    for i in range(4):
+        nat_ref[pl.ds(yy, 8, stride=4), :] = nat
+    out_rank = pltpu.make_async_copy(nat_ref, r_hbm, sem.at[8])
+    out_rank.start()
+
+    for i in range(8):
         out(i).wait()
+    out_rank.wait()
 
 
 def solution(mesh):
@@ -353,10 +383,10 @@
             out_specs=(pl.BlockSpec(memory_space=VM),) * 3,
             scratch_shapes=[
                 VM((16, NZ, 16, 512), BF16), VM((512, 1024), BF16), VM((512, 1024), BF16),
-                pltpu.SMEM((1,), F32), VM((8, 256, 1024), BF16), VM((8, 256, 1024), BF16), VM((512, 512), F32), VM((512, 512), F32),
+                pltpu.SMEM((1,), F32), VM((9, 256, 1024), BF16), VM((9, 256, 1024), BF16), VM((512, 512), F32), VM((512, 512), F32),
                 VM((32, 4, 128), F32), VM((32, 4, 128), F32), VM((NZ, 4, 128), F32), VM((32, 4, 128), F32),
                 D((4,)), D((3,)), D((1,)), D((6,)), D((1,)), D((12,)), D((1,)), D((12,)),
-                D((1,)), D((8,)), D((3,)), D((3,)),
+                D((1,)), D((9,)), D((3,)), D((3,)),
             ],
             compiler_params=pltpu.CompilerParams(collective_id=0, has_side_effects=True,
                                                  vmem_limit_bytes=48 * 1024 * 1024),
@@ -365,8 +395,8 @@
             normalise_kernel,
             out_shape=(jax.ShapeDtypeStruct((NZ, 32, 16, 512), BF16), jax.ShapeDtypeStruct((32, 128), F32)),
             in_specs=[pl.BlockSpec(memory_space=VM)] * 3,
-            out_specs=(pl.BlockSpec(memory_space=pl.ANY), pl.BlockSpec(memory_space=VM)),
-            scratch_shapes=[VM((NZ, 32, 16, 512), BF16), D((4,))],
+            out_specs=(pl.BlockSpec(memory_space=pl.ANY),) * 2,
+            scratch_shapes=[VM((NZ, 32, 16, 512), BF16), VM((32, 128), F32), D((9,))],
             compiler_params=pltpu.CompilerParams(vmem_limit_bytes=24 * 1024 * 1024),
         )(e, fac, rank)
         return prob.reshape(4096, 512), rank.reshape(4096)

time: 51.7 us -> 52.3 us (1.012)
  Pallas kernels: 50.4 us -> 51 us
    pallas_call x1, Pallas kernels: 47.5 us -> 48.8 us  [per_device(): pl.pallas_call(gather_score_kernel, out_shape=(VM((32, 128, 512), F32), V...]
    pallas_call x1, Pallas kernels: 2.85 us -> 2.22 us  [per_device(): pl.pallas_call(normalise_kernel, out_shape=(jax.ShapeDtypeStruct((NZ, 32,...]
where the time goes in v9:
time: 52.3 us
  Pallas kernels  51 us (98%)
  between operations  1.28 us (2%)
    pallas_call x1, Pallas kernels, per_device(): pl.pallas_call(gather_score_kernel, out_shape=(VM((32, 128, 512), F32), V...  48.8 us
    pallas_call x1, Pallas kernels, per_device(): pl.pallas_call(normalise_kernel, out_shape=(jax.ShapeDtypeStruct((NZ, 32,...  2.22 us

profile of v9, /device:TPU:1, one launch (start us, length us, event | category | flops | bytes accessed | tf_op | source)
XLA Modules:
  0.0 52.3 jit_solution(15464120804943503212)
XLA Ops:
  1.3 48.8 %shard_map.59 = (f32[32,128,512]{2,1,0:T(8,128)S(1)}, f32[32,128]{1,0:T(8,128)S(1)}, f32[32,128]{1,0:T(8,128)S(1)}) custom-call(bf16[16,512]{1,0:T(8,128)(2,1)} %x_hbm.1, bf16[512,1024]{1,0:T(8,128)(2,1)} %w_hbm.1, bf16[512,1024]{1,0:T(8,128)(2,1)} %g_hbm.1, f32[1]{0:T(128)S(6)} %copy.6.t_hbm), custom_call_target="tpu_custom_call" | custom-call | tf_op jit(solution)/shard_map/pallas_call | solution.py:379
  50.0 2.2 %shard_map.60 = (bf16[8,32,16,512]{3,2,1,0:T(8,128)(2,1)}, f32[32,128]{1,0:T(8,128)}) custom-call(f32[32,128,512]{2,1,0:T(8,128)S(1)} %get-tuple-element.7.e_ref, f32[32,128]{1,0:T(8,128)S(1)} %get-tuple-element.8.fac_ref, f32[32,128]{1,0:T(8,128)S(1)} %get-tuple-element.9.rank_ref), custom_call_target="tpu_custom_call" | custom-call | tf_op jit(solution)/shard_map/pallas_call | solution.py:394

commit v10 on v8

--- a/solution.py
+++ b/solution.py
@@ -311,13 +311,13 @@
         sent(done.at[0:31], s_send.at[2])
 
 
-def normalise_kernel(e_ref, fac_ref, rank_ref, p_hbm, r_ref, buf, sem):
+def normalise_kernel(e_ref, fac_ref, rank_ref, p_hbm, r_hbm, buf, nat_ref, sem):
     def out(i):
-        return pltpu.make_async_copy(buf.at[:, pl.ds(8 * i, 8)], p_hbm.at[:, pl.ds(8 * i, 8)], sem.at[i])
+        return pltpu.make_async_copy(buf.at[:, pl.ds(4 * i, 4)], p_hbm.at[:, pl.ds(4 * i, 4)], sem.at[i])
 
     def body(i, carry):
-        for j in range(8):
-            gq = i * 8 + j
+        for j in range(4):
+            gq = i * 4 + j
             f = jnp.broadcast_to(fac_ref[pl.ds(gq, 1), :], (128, 128)).T
             ev = e_ref[gq]
             p = jnp.concatenate([ev[:, b * 128:(b + 1) * 128] * f for b in range(4)], axis=1)
@@ -325,7 +325,7 @@
         out(i).start()
         return carry
 
-    lax.fori_loop(0, 4, body, 0)
+    lax.fori_loop(0, 8, body, 0)
 
     lane = lax.broadcasted_iota(jnp.int32, (8, 128), 1) // 16
     sub = lax.broadcasted_iota(jnp.int32, (8, 128), 0)
@@ -335,10 +335,13 @@
         for d in range(1, 8):
             moved = pltpu.roll(pltpu.roll(r, 16 * d, 1), 8 - d, 0)
             nat = jnp.where(lax.rem(lane - sub + 8, 8) == d, moved, nat)
-        r_ref[pl.ds(yy, 8, stride=4), :] = nat
-
-    for i in range(4):
+        nat_ref[pl.ds(yy, 8, stride=4), :] = nat
+    out_rank = pltpu.make_async_copy(nat_ref, r_hbm, sem.at[8])
+    out_rank.start()
+
+    for i in range(8):
         out(i).wait()
+    out_rank.wait()
 
 
 def solution(mesh):
@@ -365,8 +368,8 @@
             normalise_kernel,
             out_shape=(jax.ShapeDtypeStruct((NZ, 32, 16, 512), BF16), jax.ShapeDtypeStruct((32, 128), F32)),
             in_specs=[pl.BlockSpec(memory_space=VM)] * 3,
-            out_specs=(pl.BlockSpec(memory_space=pl.ANY), pl.BlockSpec(memory_space=VM)),
-            scratch_shapes=[VM((NZ, 32, 16, 512), BF16), D((4,))],
+            out_specs=(pl.BlockSpec(memory_space=pl.ANY),) * 2,
+            scratch_shapes=[VM((NZ, 32, 16, 512), BF16), VM((32, 128), F32), D((9,))],
             compiler_params=pltpu.CompilerParams(vmem_limit_bytes=24 * 1024 * 1024),
         )(e, fac, rank)
         return prob.reshape(4096, 512), rank.reshape(4096)

time: 51.7 us -> 51.1 us (0.988)
  Pallas kernels: 50.4 us -> 49.7 us
    pallas_call x1, Pallas kernels: 2.85 us -> 2.22 us  [per_device(): pl.pallas_call(normalise_kernel, out_shape=(jax.ShapeDtypeStruct((NZ, 32,...]
where the time goes in v10:
time: 51.1 us; the launch traced here: 51 us
  Pallas kernels  49.7 us (97%)
  between operations  1.28 us (3%)
    pallas_call x1, Pallas kernels, per_device(): pl.pallas_call(gather_score_kernel, out_shape=(VM((32, 128, 512), F32), V...  47.5 us
    pallas_call x1, Pallas kernels, per_device(): pl.pallas_call(normalise_kernel, out_shape=(jax.ShapeDtypeStruct((NZ, 32,...  2.22 us

profile of v10, /device:TPU:1, one launch (start us, length us, event | category | flops | bytes accessed | tf_op | source)
XLA Modules:
  0.0 51.0 jit_solution(11978257837526772482)
XLA Ops:
  1.3 47.5 %shard_map.59 = (f32[32,128,512]{2,1,0:T(8,128)S(1)}, f32[32,128]{1,0:T(8,128)S(1)}, f32[32,128]{1,0:T(8,128)S(1)}) custom-call(bf16[16,512]{1,0:T(8,128)(2,1)} %x_hbm.1, bf16[512,1024]{1,0:T(8,128)(2,1)} %w_hbm.1, bf16[512,1024]{1,0:T(8,128)(2,1)} %g_hbm.1, f32[1]{0:T(128)S(6)} %copy.6.t_hbm), custom_call_target="tpu_custom_call" | custom-call | tf_op jit(solution)/shard_map/pallas_call | solution.py:352
  48.8 2.2 %shard_map.60 = (bf16[8,32,16,512]{3,2,1,0:T(8,128)(2,1)}, f32[32,128]{1,0:T(8,128)}) custom-call(f32[32,128,512]{2,1,0:T(8,128)S(1)} %get-tuple-element.7.e_ref, f32[32,128]{1,0:T(8,128)S(1)} %get-tuple-element.8.fac_ref, f32[32,128]{1,0:T(8,128)S(1)} %get-tuple-element.9.rank_ref), custom_call_target="tpu_custom_call" | custom-call | tf_op jit(solution)/shard_map/pallas_call | solution.py:367

commit v11 on v9

--- a/solution.py
+++ b/solution.py
@@ -21,7 +21,7 @@
 def gather_score_kernel(x_hbm, w_hbm, g_hbm, t_hbm,
                         e_ref, fac_ref, rank_ref,
                         xs, wv, gv, tv, qown, qsib, da, db, stat, part, zpart, done,
-                        in_sem, a_sem, y_send, y_recv, r_send, r_recv, l_send, l_recv,
+                        in_sem, a_sem, f_sem, y_send, y_recv, r_send, r_recv, l_send, l_recv,
                         q_send, q_recv, s_send, s_recv):
     me = lax.axis_index("ga")
     c = lax.rem(me, NC)
@@ -60,9 +60,11 @@
     right = dev_lm(z, lax.rem(ll + 1, 4), ml)
     left = dev_lm(z, lax.rem(ll + 3, 4), ml)
 
+    across = dev_lm(z, lax.rem(ll + 2, 4), ml)
+
     barrier = pltpu.get_barrier_semaphore()
     with scope("barrier"):
-        peers = [sib, right, left, m_next, m_prev] + z_peers
+        peers = [sib, right, left, m_next, m_prev, across] + z_peers
         for p in peers:
             pl.semaphore_signal(barrier, inc=1, device_id=(p,), device_id_type=MESH)
         pl.semaphore_wait(barrier, len(peers))
@@ -73,6 +75,8 @@
     for d in FAR_FIRST:
         same = lax.rem(z + d, NZ) // 4 == near
         rcopy(own, own, a_sem.at[0], a_sem.at[jnp.where(same, 1, 2)], z_peers[d - 1]).start()
+
+    rcopy(own, own, f_sem.at[0], f_sem.at[1], across).start()
 
     OFF = (0, 1, 3, 2)
 
@@ -101,6 +105,14 @@
         to_mid(0, h, h, m_prev).start()
         to_mid(0, h, 2 + h, m_next).start()
         round_ring(0, h)
+
+    opposite = xs.at[column(lf, ml), z]
+    rcopy(opposite, opposite, f_sem.at[0], f_sem.at[1], sib).wait_recv()
+    for d in FAR_FIRST:
+        rcopy(opposite, opposite, f_sem.at[0], f_sem.at[2], z_peers[d - 1]).start()
+
+    def across_column():
+        rcopy(xs.at[0, 0:7], xs.at[0, 0:7], f_sem.at[0], f_sem.at[2], sib).wait_recv()
 
     def mid_columns():
         with scope("second"):
@@ -127,7 +139,7 @@
     def from_left(j):
         for h in range(2):
             to_right(lm, j, h).wait_recv()
-            if j < 2:
+            if j == 1:
                 to_right(lm, j, h, 1).start()
 
     def from_right(j):
@@ -144,28 +156,25 @@
         for h in range(2):
             to_left(lf, j, h, 1).wait_recv()
 
-    UNITS = (((0, 0),), ((0, 1), (0, 3)), ((3, 0), (1, 0)), ((0, 2), (3, 1)), ((1, 1), (3, 3)),
-             ((1, 3), (3, 2)), ((1, 2), (2, 0)), ((2, 1), (2, 3)), ((2, 2),))
+    UNITS = (((0, 0), (0, 1)), ((3, 0), (1, 0)), ((0, 3), (2, 0)), ((0, 2),), ((3, 1), (1, 1)),
+             ((3, 3), (1, 3)), ((3, 2), (1, 2)), ((2, 1), (2, 3)), ((2, 2),))
 
     def unit_of(lc, mc, u):
         return [(lax.rem(lc + a, 4), lax.rem(mc + b, 4)) for a, b in UNITS[u]]
 
     def events(k):
-        if k == 2:
+        if k == 0:
+            mid_columns()
+        if k == 1:
             from_left(0)
             from_right(0)
+        if k == 2:
+            across_column()
         if k == 3:
             far_column()
-            from_left(1)
-        if k == 4:
-            from_right(1)
-            from_left(2)
-        if k == 5:
-            from_right(2)
-            from_left(3)
-        if k == 6:
-            from_right(3)
-            far_left(0)
+        if 4 <= k <= 6:
+            from_left(k - 3)
+            from_right(k - 3)
         if k == 7:
             far_left(1)
             far_right(2)
@@ -259,7 +268,7 @@
         if k < LAST:
             to_sib(k).start()
 
-    SENDS = {6: ((0, 1, 2, 3), (1,)), 7: ((4,), (2, 3)), 8: ((5, 6), (0, 4, 5)), 9: ((7,), (6,)), 10: ((8,), (7,)),
+    SENDS = {6: ((0, 1, 2, 3), (2,)), 7: ((4,), (1, 3)), 8: ((5, 6), (0, 4, 5)), 9: ((7,), (6,)), 10: ((8,), (7,)),
              11: ((), (8,))}
 
     def sends(k):
@@ -270,9 +279,7 @@
             for gq in groups_sib(u):
                 send_group(gq)
 
-    step(0)
-    mid_columns()
-    for k in range(1, LAST + 1):
+    for k in range(LAST + 1):
         step(k)
         if k in SENDS:
             sends(k)
@@ -330,7 +337,8 @@
     with scope("drain"):
         sent(xs.at[0, 0:7], a_sem.at[0])
         sent(xs.at[0:3], y_send.at[0])
-        sent(xs.at[0:6], r_send.at[0])
+        sent(xs.at[0], f_sem.at[0])
+        sent(xs.at[0:5], r_send.at[0])
         sent(xs.at[0:6], l_send.at[0])
         sent(qown.at[0:8], q_send.at[0])
         sent(part.at[0:31], s_send.at[0])
@@ -385,7 +393,7 @@
                 VM((16, NZ, 16, 512), BF16), VM((512, 1024), BF16), VM((512, 1024), BF16),
                 pltpu.SMEM((1,), F32), VM((9, 256, 1024), BF16), VM((9, 256, 1024), BF16), VM((512, 512), F32), VM((512, 512), F32),
                 VM((32, 4, 128), F32), VM((32, 4, 128), F32), VM((NZ, 4, 128), F32), VM((32, 4, 128), F32),
-                D((4,)), D((3,)), D((1,)), D((6,)), D((1,)), D((12,)), D((1,)), D((12,)),
+                D((4,)), D((3,)), D((3,)), D((1,)), D((6,)), D((1,)), D((12,)), D((1,)), D((12,)),
                 D((1,)), D((9,)), D((3,)), D((3,)),
             ],
             compiler_params=pltpu.CompilerParams(collective_id=0, has_side_effects=True,

time: 52.3 us -> 50.8 us (0.971)
  Pallas kernels: 51 us -> 49.4 us
    pallas_call x1, Pallas kernels: 48.8 us -> 47.2 us  [per_device(): pl.pallas_call(gather_score_kernel, out_shape=(VM((32, 128, 512), F32), V...]
where the time goes in v11:
time: 50.8 us; the launch traced here: 50.7 us
  Pallas kernels  49.4 us (97%)
  between operations  1.28 us (3%)
    pallas_call x1, Pallas kernels, per_device(): pl.pallas_call(gather_score_kernel, out_shape=(VM((32, 128, 512), F32), V...  47.2 us
    pallas_call x1, Pallas kernels, per_device(): pl.pallas_call(normalise_kernel, out_shape=(jax.ShapeDtypeStruct((NZ, 32,...  2.22 us

profile of v11, /device:TPU:1, one launch (start us, length us, event | category | flops | bytes accessed | tf_op | source)
XLA Modules:
  0.0 50.7 jit_solution(6381210011343306044)
XLA Ops:
  1.3 47.2 %shard_map.59 = (f32[32,128,512]{2,1,0:T(8,128)S(1)}, f32[32,128]{1,0:T(8,128)S(1)}, f32[32,128]{1,0:T(8,128)S(1)}) custom-call(bf16[16,512]{1,0:T(8,128)(2,1)} %x_hbm.1, bf16[512,1024]{1,0:T(8,128)(2,1)} %w_hbm.1, bf16[512,1024]{1,0:T(8,128)(2,1)} %g_hbm.1, f32[1]{0:T(128)S(6)} %copy.6.t_hbm), custom_call_target="tpu_custom_call" | custom-call | tf_op jit(solution)/shard_map/pallas_call | solution.py:387
  48.5 2.2 %shard_map.60 = (bf16[8,32,16,512]{3,2,1,0:T(8,128)(2,1)}, f32[32,128]{1,0:T(8,128)}) custom-call(f32[32,128,512]{2,1,0:T(8,128)S(1)} %get-tuple-element.7.e_ref, f32[32,128]{1,0:T(8,128)S(1)} %get-tuple-element.8.fac_ref, f32[32,128]{1,0:T(8,128)S(1)} %get-tuple-element.9.rank_ref), custom_call_target="tpu_custom_call" | custom-call | tf_op jit(solution)/shard_map/pallas_call | solution.py:402

commit v12 on v11

--- a/solution.py
+++ b/solution.py
@@ -254,18 +254,18 @@
         with scope("sibwait"):
             for u in us:
                 to_sib(u).wait_recv()
-        if k == LAST:
+        if k >= LAST - 1:
             with scope("project"):
                 project(k)
             to_sib(k).start()
         with scope("compute"):
             if k >= 2:
                 soften(before, groups_of(*scored(k - 1)))
-            if k < LAST:
+            if k < LAST - 1:
                 project(k)
             if uo or us:
                 dots(now, uo, us)
-        if k < LAST:
+        if k < LAST - 1:
             to_sib(k).start()
 
     SENDS = {6: ((0, 1, 2, 3), (2,)), 7: ((4,), (1, 3)), 8: ((5, 6), (0, 4, 5)), 9: ((7,), (6,)), 10: ((8,), (7,)),

time: 50.8 us -> 50.8 us (level)
  no operation moved by 1% of the time
where the time goes in v12:
time: 50.8 us; the launch traced here: 50.7 us
  Pallas kernels  49.4 us (97%)
  between operations  1.28 us (3%)
    pallas_call x1, Pallas kernels, per_device(): pl.pallas_call(gather_score_kernel, out_shape=(VM((32, 128, 512), F32), V...  47.2 us
    pallas_call x1, Pallas kernels, per_device(): pl.pallas_call(normalise_kernel, out_shape=(jax.ShapeDtypeStruct((NZ, 32,...  2.22 us

profile of v12, /device:TPU:1, one launch (start us, length us, event | category | flops | bytes accessed | tf_op | source)
XLA Modules:
  0.0 50.7 jit_solution(6206296837783297707)
XLA Ops:
  1.3 47.2 %shard_map.59 = (f32[32,128,512]{2,1,0:T(8,128)S(1)}, f32[32,128]{1,0:T(8,128)S(1)}, f32[32,128]{1,0:T(8,128)S(1)}) custom-call(bf16[16,512]{1,0:T(8,128)(2,1)} %x_hbm.1, bf16[512,1024]{1,0:T(8,128)(2,1)} %w_hbm.1, bf16[512,1024]{1,0:T(8,128)(2,1)} %g_hbm.1, f32[1]{0:T(128)S(6)} %copy.6.t_hbm), custom_call_target="tpu_custom_call" | custom-call | tf_op jit(solution)/shard_map/pallas_call | solution.py:387
  48.4 2.2 %shard_map.60 = (bf16[8,32,16,512]{3,2,1,0:T(8,128)(2,1)}, f32[32,128]{1,0:T(8,128)}) custom-call(f32[32,128,512]{2,1,0:T(8,128)S(1)} %get-tuple-element.7.e_ref, f32[32,128]{1,0:T(8,128)S(1)} %get-tuple-element.8.fac_ref, f32[32,128]{1,0:T(8,128)S(1)} %get-tuple-element.9.rank_ref), custom_call_target="tpu_custom_call" | custom-call | tf_op jit(solution)/shard_map/pallas_call | solution.py:402
